TPU v7x, 16 devices: a whole 2x2x2 slice. The times are simulated.
16 devices in a mesh: dp: 2 (over z), cp: 8 (over y, x, core).
Axes of the slice: x: 2, y: 2, z: 2, core: 2. Of those that a mesh axis runs over, the one named last changes fastest.
Arguments:
- hidden: bfloat16 [8, 2048, 6656], P('dp', 'cp')
- positions: int32 [2048], P('cp')
- w_q: bfloat16 [6656, 6656], replicated
- w_k: bfloat16 [6656, 6656], replicated
- w_v: bfloat16 [6656, 6656], replicated
- w_o: bfloat16 [6656, 6656], replicated
Outputs:
- output 1: bfloat16 [8, 2048, 6656], P('dp', 'cp')
- output 2: float32 [52], replicated
- output 3: bfloat16 [6656, 6656], replicated
- output 4: bfloat16 [6656, 6656], replicated
All inputs are finite; a program needn't handle non-finite values.
Results may differ from a plain program's by a relative error of at most 0.00771897.
Values are sent between devices in bfloat16 or wider.
A program may use at most 2.25 GiB of HBM per device.

v0:
```python
import jax
import jax.numpy as jnp
from jax import lax
from jax.sharding import PartitionSpec as P

HEAD_DIM = 128
TAU_CLIP = 100.0
ROPE_THETA = 50000.0


def rope_tables(pos_ids):
    half_dim = HEAD_DIM // 2
    inv_freq = jnp.float32(ROPE_THETA) ** (-jnp.arange(half_dim, dtype=jnp.float32) * (2.0 / HEAD_DIM))
    angle = pos_ids.astype(jnp.float32)[:, None] * inv_freq[None, :]
    return jnp.cos(angle)[None, :, None, :], jnp.sin(angle)[None, :, None, :]


def rope_rotate(tensor, cos_t, sin_t):
    half_dim = HEAD_DIM // 2
    lead_half = tensor[..., :half_dim]
    tail_half = tensor[..., half_dim:]
    return jnp.concatenate([lead_half * cos_t - tail_half * sin_t, tail_half * cos_t + lead_half * sin_t], axis=-1)


def project_heads(hidden, pos_ids, w_q, w_k, w_v):
    batch_n, seq_n, _ = hidden.shape
    head_shape = (batch_n, seq_n, w_q.shape[1] // HEAD_DIM, HEAD_DIM)
    cos_t, sin_t = rope_tables(pos_ids)
    q_heads = rope_rotate(jnp.dot(hidden, w_q, preferred_element_type=jnp.float32).reshape(head_shape), cos_t, sin_t).astype(jnp.bfloat16)
    k_heads = rope_rotate(jnp.dot(hidden, w_k, preferred_element_type=jnp.float32).reshape(head_shape), cos_t, sin_t).astype(jnp.bfloat16)
    v_heads = jnp.dot(hidden, w_v, preferred_element_type=jnp.float32).astype(jnp.bfloat16).reshape(head_shape)
    return q_heads, k_heads, v_heads


def empty_state(batch_n, seq_n, n_heads):
    row_shape = (batch_n, n_heads, seq_n)
    return (jnp.full(row_shape, -jnp.inf, jnp.float32), jnp.zeros(row_shape, jnp.float32),
            jnp.zeros((batch_n, seq_n, n_heads, HEAD_DIM), jnp.float32), jnp.full((n_heads,), -jnp.inf, jnp.float32))


def attend_block(q_heads, k_blk, v_blk, state, allowed):
    run_max, run_sum, out_acc, head_max = state
    scores = jnp.einsum("bqhd,bkhd->bhqk", q_heads, k_blk, preferred_element_type=jnp.float32) * (HEAD_DIM ** -0.5)
    if allowed is not None:
        scores = jnp.where(allowed, scores, -jnp.inf)
    head_max = jnp.maximum(head_max, jnp.max(scores, axis=(0, 2, 3)))
    new_max = jnp.maximum(run_max, jnp.max(scores, axis=-1))
    rescale = jnp.exp(run_max - new_max)
    prob_w = jnp.exp(scores - new_max[..., None])
    new_sum = run_sum * rescale + jnp.sum(prob_w, axis=-1)
    part_pv = jnp.einsum("bhqk,bkhd->bqhd", prob_w.astype(jnp.bfloat16), v_blk, preferred_element_type=jnp.float32)
    new_acc = out_acc * jnp.transpose(rescale, (0, 2, 1))[..., None] + part_pv
    return new_max, new_sum, new_acc, head_max


def finish_attn(state, w_o):
    run_max, run_sum, out_acc, head_max = state
    batch_n, seq_n, n_heads, _ = out_acc.shape
    attn_val = (out_acc / jnp.transpose(run_sum, (0, 2, 1))[..., None]).astype(jnp.bfloat16)
    attn_val = attn_val.reshape(batch_n, seq_n, n_heads * HEAD_DIM)
    return jnp.dot(attn_val, w_o, preferred_element_type=jnp.float32).astype(jnp.bfloat16), head_max


def clip_weights(head_max, w_q, w_k):
    factor = jnp.where(head_max > TAU_CLIP, jnp.sqrt(TAU_CLIP / head_max), 1.0)
    col_factor = jnp.repeat(factor, HEAD_DIM)[None, :]
    return (w_q.astype(jnp.float32) * col_factor).astype(jnp.bfloat16), (w_k.astype(jnp.float32) * col_factor).astype(jnp.bfloat16)


def solution(mesh):
    cp_size = mesh.shape["cp"]
    shift_pairs = [(src_rank, (src_rank + 1) % cp_size) for src_rank in range(cp_size)]

    def device_body(hidden, pos_ids, w_q, w_k, w_v, w_o):
        cp_rank = lax.axis_index("cp")
        q_heads, k_heads, v_heads = project_heads(hidden, pos_ids, w_q, w_k, w_v)
        batch_n, seq_n, n_heads, _ = q_heads.shape
        causal = lax.broadcasted_iota(jnp.int32, (seq_n, seq_n), 0) >= lax.broadcasted_iota(jnp.int32, (seq_n, seq_n), 1)
        state = attend_block(q_heads, k_heads, v_heads, empty_state(batch_n, seq_n, n_heads), causal)

        def step(step_idx, carried):
            k_blk, v_blk, attn_state = carried
            k_blk = lax.ppermute(k_blk, "cp", shift_pairs)
            v_blk = lax.ppermute(v_blk, "cp", shift_pairs)

            def use_block(state_in):
                return attend_block(q_heads, k_blk, v_blk, state_in, None)

            def skip_block(state_in):
                return state_in

            attn_state = lax.cond(step_idx <= cp_rank, use_block, skip_block, attn_state)
            return k_blk, v_blk, attn_state

        _, _, state = lax.fori_loop(1, cp_size, step, (k_heads, v_heads, state))
        attn_out, head_max = finish_attn(state, w_o)
        head_max = lax.pmax(head_max, ("dp", "cp"))
        w_q_new, w_k_new = clip_weights(head_max, w_q, w_k)
        return attn_out, head_max, w_q_new, w_k_new

    return jax.shard_map(
        device_body,
        mesh=mesh,
        in_specs=(P("dp", "cp", None), P("cp"), P(None, None), P(None, None), P(None, None), P(None, None)),
        out_specs=(P("dp", "cp", None), P(None), P(None, None), P(None, None)),
        check_vma=False,
    )
```

profile of v0, /device:TPU:0, one launch (start us, length us, event | category | flops | bytes accessed | tf_op | source)
XLA Modules:
  0.0 3746.6 jit_solution(1900107811306696009)
XLA Ops:
  0.6 109.6 %fusion.12 = f32[4,256,6656]{1,2,0:T(8,128)} fusion(bf16[4,256,6656]{2,1,0:T(8,128)(2,1)} %param.10, bf16[6656,6656]{1,0:T(8,128)(2,1)} %param.12), kind=kOutput, calls=%fused_computation.17 | convolution fusion | flops 90731184128 | bytes 129499136 | tf_op jit(solution)/shard_map/dot_general | solution.py:29
  167.6 109.7 %fusion.16 = f32[4,256,6656]{1,2,0:T(8,128)} fusion(bf16[4,256,6656]{2,1,0:T(8,128)(2,1)} %param.10, bf16[6656,6656]{1,0:T(8,128)(2,1)} %param.13), kind=kOutput, calls=%fused_computation.21 | convolution fusion | flops 90731184128 | bytes 129499136 | tf_op jit(solution)/shard_map/dot_general | solution.py:30
  333.3 54.0 %subtract_convert_fusion = (bf16[4,256,52,64]{3,1,2,0:T(8,128)(2,1)}, bf16[4,256,52,64]{3,1,2,0:T(8,128)(2,1)}, bf16[4,256,52,64]{3,1,2,0:T(8,128)(2,1)}, bf16[4,256,52,64]{3,1,2,0:T(8,128)(2,1)}) fusion(f32[4,256,52,64]{3,1,2,0:T(8,128)} %copy.40, f32[4,256,52,64]{3,1,2,0:T(8,128)} %copy.39, f32[256,64]{1,0:T(8,128)S(1)} %copy-done.1, ...), kind=kLoop, calls=%fused_computation.36 | loop fusion | flops 54525952 | bytes 81920000 | tf_op jit(solution)/shard_map/convert
  418.0 101.5 %fusion.28 = bf16[4,256,6656]{2,1,0:T(8,128)(2,1)} fusion(bf16[4,256,6656]{2,1,0:T(8,128)(2,1)} %param.10, bf16[6656,6656]{1,0:T(8,128)(2,1)} %param.14), kind=kOutput, calls=%fused_computation.42 | convolution fusion | flops 90737999872 | bytes 115867648 | tf_op jit(solution)/shard_map/dot_general | solution.py:31
  658.8 2721.9 %while.23 = (s32[]{:T(128)}, bf16[4,256,52,128]{3,1,2,0:T(8,128)(2,1)}, bf16[4,256,52,128]{3,1,2,0:T(8,128)(2,1)}, f32[4,52,256]{2,1,0:T(8,128)S(1)}, f32[4,52,2...) while((s32[]{:T(128)}, ...), condition=%wide.region_9.10_spmd, body=%wide.region_3.9_spmd.sunk | while | flops 7115796480 | bytes 425985152 | solution.py:95
  662.4 147.6 %collective-permute-done = bf16[4,256,52,128]{3,1,2,0:T(8,128)(2,1)} collective-permute-done((bf16[4,256,52,128]{3,1,2,0:T(8,128)(2,1)}, bf16[4,256,52,128]{3,1,2,0:T(8,128)(2,1)}, u32[]{:S(2)}, u32[]{:S(2)}) %collective-permute-start) | collective-permute-done | bytes 13631520 | tf_op jit(solution)/shard_map/while/body/eval_jaxpr/ppermute | solution.py:83
  810.0 146.1 %collective-permute-done.1 = bf16[4,256,52,128]{3,1,2,0:T(8,128)(2,1)} collective-permute-done((bf16[4,256,52,128]{3,1,2,0:T(8,128)(2,1)}, bf16[4,256,52,128]{3,1,2,0:T(8,128)(2,1)}, u32[]{:S(2)}, u32[]{:S(2)}) %collective-permute-start.1) | collective-permute-done | bytes 13631520 | tf_op jit(solution)/shard_map/while/body/eval_jaxpr/ppermute | solution.py:84
  976.7 86.3 %collective-permute-start = (bf16[4,256,52,128]{3,1,2,0:T(8,128)(2,1)}, bf16[4,256,52,128]{3,1,2,0:T(8,128)(2,1)}, u32[]{:S(2)}, u32[]{:S(2)}) collective-permute-start(bf16[4,256,52,128]{3,1,2,0:T(8,128)(2,1)} %get-tuple-element.350), channel_id=1, source_target_pairs={{0,1},{1,2},{2,3},{3,4},{4,5},{5,6},{6,7},{7,0},{8,9},{9,10},{10,1... | collective-permute-start | bytes 40894472 | tf_op jit(solution)/shard_map/while/body/eval_jaxpr/ppermute | solution.py:83
  1065.5 145.1 %collective-permute-done = bf16[4,256,52,128]{3,1,2,0:T(8,128)(2,1)} collective-permute-done((bf16[4,256,52,128]{3,1,2,0:T(8,128)(2,1)}, bf16[4,256,52,128]{3,1,2,0:T(8,128)(2,1)}, u32[]{:S(2)}, u32[]{:S(2)}) %collective-permute-start) | collective-permute-done | bytes 13631520 | tf_op jit(solution)/shard_map/while/body/eval_jaxpr/ppermute | solution.py:83
  1210.6 146.1 %collective-permute-done.1 = bf16[4,256,52,128]{3,1,2,0:T(8,128)(2,1)} collective-permute-done((bf16[4,256,52,128]{3,1,2,0:T(8,128)(2,1)}, bf16[4,256,52,128]{3,1,2,0:T(8,128)(2,1)}, u32[]{:S(2)}, u32[]{:S(2)}) %collective-permute-start.1) | collective-permute-done | bytes 13631520 | tf_op jit(solution)/shard_map/while/body/eval_jaxpr/ppermute | solution.py:84
  1378.8 89.9 %collective-permute-start.1 = (bf16[4,256,52,128]{3,1,2,0:T(8,128)(2,1)}, bf16[4,256,52,128]{3,1,2,0:T(8,128)(2,1)}, u32[]{:S(2)}, u32[]{:S(2)}) collective-permute-start(bf16[4,256,52,128]{3,1,2,0:T(8,128)(2,1)} %get-tuple-element.351), channel_id=1, source_target_pairs={{0,1},{1,2},{2,3},{3,4},{4,5},{5,6},{6,7},{7,0},{8,9},{9,10},{10,1... | collective-permute-start | bytes 40894472 | tf_op jit(solution)/shard_map/while/body/eval_jaxpr/ppermute | solution.py:84
  1468.7 142.6 %collective-permute-done = bf16[4,256,52,128]{3,1,2,0:T(8,128)(2,1)} collective-permute-done((bf16[4,256,52,128]{3,1,2,0:T(8,128)(2,1)}, bf16[4,256,52,128]{3,1,2,0:T(8,128)(2,1)}, u32[]{:S(2)}, u32[]{:S(2)}) %collective-permute-start) | collective-permute-done | bytes 13631520 | tf_op jit(solution)/shard_map/while/body/eval_jaxpr/ppermute | solution.py:83
  1611.3 146.1 %collective-permute-done.1 = bf16[4,256,52,128]{3,1,2,0:T(8,128)(2,1)} collective-permute-done((bf16[4,256,52,128]{3,1,2,0:T(8,128)(2,1)}, bf16[4,256,52,128]{3,1,2,0:T(8,128)(2,1)}, u32[]{:S(2)}, u32[]{:S(2)}) %collective-permute-start.1) | collective-permute-done | bytes 13631520 | tf_op jit(solution)/shard_map/while/body/eval_jaxpr/ppermute | solution.py:84
  1784.5 227.5 %collective-permute-done = bf16[4,256,52,128]{3,1,2,0:T(8,128)(2,1)} collective-permute-done((bf16[4,256,52,128]{3,1,2,0:T(8,128)(2,1)}, bf16[4,256,52,128]{3,1,2,0:T(8,128)(2,1)}, u32[]{:S(2)}, u32[]{:S(2)}) %collective-permute-start) | collective-permute-done | bytes 13631520 | tf_op jit(solution)/shard_map/while/body/eval_jaxpr/ppermute | solution.py:83
  2012.0 146.1 %collective-permute-done.1 = bf16[4,256,52,128]{3,1,2,0:T(8,128)(2,1)} collective-permute-done((bf16[4,256,52,128]{3,1,2,0:T(8,128)(2,1)}, bf16[4,256,52,128]{3,1,2,0:T(8,128)(2,1)}, u32[]{:S(2)}, u32[]{:S(2)}) %collective-permute-start.1) | collective-permute-done | bytes 13631520 | tf_op jit(solution)/shard_map/while/body/eval_jaxpr/ppermute | solution.py:84
  2178.7 233.9 %collective-permute-done = bf16[4,256,52,128]{3,1,2,0:T(8,128)(2,1)} collective-permute-done((bf16[4,256,52,128]{3,1,2,0:T(8,128)(2,1)}, bf16[4,256,52,128]{3,1,2,0:T(8,128)(2,1)}, u32[]{:S(2)}, u32[]{:S(2)}) %collective-permute-start) | collective-permute-done | bytes 13631520 | tf_op jit(solution)/shard_map/while/body/eval_jaxpr/ppermute | solution.py:83
  2412.6 146.1 %collective-permute-done.1 = bf16[4,256,52,128]{3,1,2,0:T(8,128)(2,1)} collective-permute-done((bf16[4,256,52,128]{3,1,2,0:T(8,128)(2,1)}, bf16[4,256,52,128]{3,1,2,0:T(8,128)(2,1)}, u32[]{:S(2)}, u32[]{:S(2)}) %collective-permute-start.1) | collective-permute-done | bytes 13631520 | tf_op jit(solution)/shard_map/while/body/eval_jaxpr/ppermute | solution.py:84
  2579.4 233.9 %collective-permute-done = bf16[4,256,52,128]{3,1,2,0:T(8,128)(2,1)} collective-permute-done((bf16[4,256,52,128]{3,1,2,0:T(8,128)(2,1)}, bf16[4,256,52,128]{3,1,2,0:T(8,128)(2,1)}, u32[]{:S(2)}, u32[]{:S(2)}) %collective-permute-start) | collective-permute-done | bytes 13631520 | tf_op jit(solution)/shard_map/while/body/eval_jaxpr/ppermute | solution.py:83
  2813.3 146.1 %collective-permute-done.1 = bf16[4,256,52,128]{3,1,2,0:T(8,128)(2,1)} collective-permute-done((bf16[4,256,52,128]{3,1,2,0:T(8,128)(2,1)}, bf16[4,256,52,128]{3,1,2,0:T(8,128)(2,1)}, u32[]{:S(2)}, u32[]{:S(2)}) %collective-permute-start.1) | collective-permute-done | bytes 13631520 | tf_op jit(solution)/shard_map/while/body/eval_jaxpr/ppermute | solution.py:84
  2980.0 233.9 %collective-permute-done = bf16[4,256,52,128]{3,1,2,0:T(8,128)(2,1)} collective-permute-done((bf16[4,256,52,128]{3,1,2,0:T(8,128)(2,1)}, bf16[4,256,52,128]{3,1,2,0:T(8,128)(2,1)}, u32[]{:S(2)}, u32[]{:S(2)}) %collective-permute-start) | collective-permute-done | bytes 13631520 | tf_op jit(solution)/shard_map/while/body/eval_jaxpr/ppermute | solution.py:83
  3213.9 146.1 %collective-permute-done.1 = bf16[4,256,52,128]{3,1,2,0:T(8,128)(2,1)} collective-permute-done((bf16[4,256,52,128]{3,1,2,0:T(8,128)(2,1)}, bf16[4,256,52,128]{3,1,2,0:T(8,128)(2,1)}, u32[]{:S(2)}, u32[]{:S(2)}) %collective-permute-start.1) | collective-permute-done | bytes 13631520 | tf_op jit(solution)/shard_map/while/body/eval_jaxpr/ppermute | solution.py:84
  3417.5 97.9 %fusion.31 = bf16[4,256,6656]{2,1,0:T(8,128)(2,1)} fusion(bf16[4,256,6656]{1,2,0:T(8,128)(2,1)S(1)} %bitcast.45, bf16[6656,6656]{1,0:T(8,128)(2,1)} %param.15), kind=kOutput, calls=%fused_computation.43 | convolution fusion | flops 90737999872 | bytes 115867648 | tf_op jit(solution)/shard_map/dot_general | solution.py:61
  3515.5 116.2 %pmax.7 = f32[52]{0:T(128)S(1)} all-reduce(f32[52]{0:T(128)S(1)} %get-tuple-element.203), channel_id=1, replica_groups=mesh['dp'=2,'cp'=8] {'dp','cp'}, use_global_device_ids=true, to_apply=%region_10.11 | all-reduce | flops 52 | bytes 416 | tf_op jit(solution)/shard_map/pmax | solution.py:97
  3631.7 114.5 %multiply_convert_fusion = (bf16[6656,6656]{1,0:T(8,128)(2,1)}, bf16[6656,6656]{1,0:T(8,128)(2,1)}) fusion(bf16[6656,6656]{1,0:T(8,128)(2,1)} %param.13, f32[6656]{0:T(1024)S(1)} %broadcast_bitcast_fusion, bf16[6656,6656]{1,0:T(8,128)(2,1)} %param.12), kind=kLoop, calls=%fused_computation.13 | loop fusion | flops 265814016 | bytes 354445312 | tf_op jit(solution)/shard_map/convert_element_type | solution.py:67
  (63 shorter events, 478.8 us)
Async XLA Ops:
  147.2 19.1 copy-start.2
  314.1 19.2 copy-start
  314.1 19.2 copy-start.1
  659.0 151.0 %collective-permute-start = (bf16[4,256,52,128]{3,1,2,0:T(8,128)(2,1)}, bf16[4,256,52,128]{3,1,2,0:T(8,128)(2,1)}, u32[]{:S(2)}, u32[]{:S(2)}) collective-permute-start(bf16[4,256,52,128]{3,1,2,0:T(8,128)(2,1)} %get-tuple-element.350), channel_id=1, source_target_pairs={{0,1},{1,2},{2,3},{3,4},{4,5},{5,6},{6,7},{7,0},{8,9},{9,10},{10,1... | collective-permute-start | bytes 40894472 | tf_op jit(solution)/shard_map/while/body/eval_jaxpr/ppermute | solution.py:83
  659.8 296.2 %collective-permute-start.1 = (bf16[4,256,52,128]{3,1,2,0:T(8,128)(2,1)}, bf16[4,256,52,128]{3,1,2,0:T(8,128)(2,1)}, u32[]{:S(2)}, u32[]{:S(2)}) collective-permute-start(bf16[4,256,52,128]{3,1,2,0:T(8,128)(2,1)} %get-tuple-element.351), channel_id=1, source_target_pairs={{0,1},{1,2},{2,3},{3,4},{4,5},{5,6},{6,7},{7,0},{8,9},{9,10},{10,1... | collective-permute-start | bytes 40894472 | tf_op jit(solution)/shard_map/while/body/eval_jaxpr/ppermute | solution.py:84
  976.7 233.9 %collective-permute-start = (bf16[4,256,52,128]{3,1,2,0:T(8,128)(2,1)}, bf16[4,256,52,128]{3,1,2,0:T(8,128)(2,1)}, u32[]{:S(2)}, u32[]{:S(2)}) collective-permute-start(bf16[4,256,52,128]{3,1,2,0:T(8,128)(2,1)} %get-tuple-element.350), channel_id=1, source_target_pairs={{0,1},{1,2},{2,3},{3,4},{4,5},{5,6},{6,7},{7,0},{8,9},{9,10},{10,1... | collective-permute-start | bytes 40894472 | tf_op jit(solution)/shard_map/while/body/eval_jaxpr/ppermute | solution.py:83
  1063.0 293.7 %collective-permute-start.1 = (bf16[4,256,52,128]{3,1,2,0:T(8,128)(2,1)}, bf16[4,256,52,128]{3,1,2,0:T(8,128)(2,1)}, u32[]{:S(2)}, u32[]{:S(2)}) collective-permute-start(bf16[4,256,52,128]{3,1,2,0:T(8,128)(2,1)} %get-tuple-element.351), channel_id=1, source_target_pairs={{0,1},{1,2},{2,3},{3,4},{4,5},{5,6},{6,7},{7,0},{8,9},{9,10},{10,1... | collective-permute-start | bytes 40894472 | tf_op jit(solution)/shard_map/while/body/eval_jaxpr/ppermute | solution.py:84
  1377.4 233.9 %collective-permute-start = (bf16[4,256,52,128]{3,1,2,0:T(8,128)(2,1)}, bf16[4,256,52,128]{3,1,2,0:T(8,128)(2,1)}, u32[]{:S(2)}, u32[]{:S(2)}) collective-permute-start(bf16[4,256,52,128]{3,1,2,0:T(8,128)(2,1)} %get-tuple-element.350), channel_id=1, source_target_pairs={{0,1},{1,2},{2,3},{3,4},{4,5},{5,6},{6,7},{7,0},{8,9},{9,10},{10,1... | collective-permute-start | bytes 40894472 | tf_op jit(solution)/shard_map/while/body/eval_jaxpr/ppermute | solution.py:83
  1378.8 378.6 %collective-permute-start.1 = (bf16[4,256,52,128]{3,1,2,0:T(8,128)(2,1)}, bf16[4,256,52,128]{3,1,2,0:T(8,128)(2,1)}, u32[]{:S(2)}, u32[]{:S(2)}) collective-permute-start(bf16[4,256,52,128]{3,1,2,0:T(8,128)(2,1)} %get-tuple-element.351), channel_id=1, source_target_pairs={{0,1},{1,2},{2,3},{3,4},{4,5},{5,6},{6,7},{7,0},{8,9},{9,10},{10,1... | collective-permute-start | bytes 40894472 | tf_op jit(solution)/shard_map/while/body/eval_jaxpr/ppermute | solution.py:84
  1778.0 233.9 %collective-permute-start = (bf16[4,256,52,128]{3,1,2,0:T(8,128)(2,1)}, bf16[4,256,52,128]{3,1,2,0:T(8,128)(2,1)}, u32[]{:S(2)}, u32[]{:S(2)}) collective-permute-start(bf16[4,256,52,128]{3,1,2,0:T(8,128)(2,1)} %get-tuple-element.350), channel_id=1, source_target_pairs={{0,1},{1,2},{2,3},{3,4},{4,5},{5,6},{6,7},{7,0},{8,9},{9,10},{10,1... | collective-permute-start | bytes 40894472 | tf_op jit(solution)/shard_map/while/body/eval_jaxpr/ppermute | solution.py:83
  1782.0 376.1 %collective-permute-start.1 = (bf16[4,256,52,128]{3,1,2,0:T(8,128)(2,1)}, bf16[4,256,52,128]{3,1,2,0:T(8,128)(2,1)}, u32[]{:S(2)}, u32[]{:S(2)}) collective-permute-start(bf16[4,256,52,128]{3,1,2,0:T(8,128)(2,1)} %get-tuple-element.351), channel_id=1, source_target_pairs={{0,1},{1,2},{2,3},{3,4},{4,5},{5,6},{6,7},{7,0},{8,9},{9,10},{10,1... | collective-permute-start | bytes 40894472 | tf_op jit(solution)/shard_map/while/body/eval_jaxpr/ppermute | solution.py:84
  2178.7 233.9 %collective-permute-start = (bf16[4,256,52,128]{3,1,2,0:T(8,128)(2,1)}, bf16[4,256,52,128]{3,1,2,0:T(8,128)(2,1)}, u32[]{:S(2)}, u32[]{:S(2)}) collective-permute-start(bf16[4,256,52,128]{3,1,2,0:T(8,128)(2,1)} %get-tuple-element.350), channel_id=1, source_target_pairs={{0,1},{1,2},{2,3},{3,4},{4,5},{5,6},{6,7},{7,0},{8,9},{9,10},{10,1... | collective-permute-start | bytes 40894472 | tf_op jit(solution)/shard_map/while/body/eval_jaxpr/ppermute | solution.py:83
  2178.7 380.0 %collective-permute-start.1 = (bf16[4,256,52,128]{3,1,2,0:T(8,128)(2,1)}, bf16[4,256,52,128]{3,1,2,0:T(8,128)(2,1)}, u32[]{:S(2)}, u32[]{:S(2)}) collective-permute-start(bf16[4,256,52,128]{3,1,2,0:T(8,128)(2,1)} %get-tuple-element.351), channel_id=1, source_target_pairs={{0,1},{1,2},{2,3},{3,4},{4,5},{5,6},{6,7},{7,0},{8,9},{9,10},{10,1... | collective-permute-start | bytes 40894472 | tf_op jit(solution)/shard_map/while/body/eval_jaxpr/ppermute | solution.py:84
  2579.4 233.9 %collective-permute-start = (bf16[4,256,52,128]{3,1,2,0:T(8,128)(2,1)}, bf16[4,256,52,128]{3,1,2,0:T(8,128)(2,1)}, u32[]{:S(2)}, u32[]{:S(2)}) collective-permute-start(bf16[4,256,52,128]{3,1,2,0:T(8,128)(2,1)} %get-tuple-element.350), channel_id=1, source_target_pairs={{0,1},{1,2},{2,3},{3,4},{4,5},{5,6},{6,7},{7,0},{8,9},{9,10},{10,1... | collective-permute-start | bytes 40894472 | tf_op jit(solution)/shard_map/while/body/eval_jaxpr/ppermute | solution.py:83
  2579.4 380.0 %collective-permute-start.1 = (bf16[4,256,52,128]{3,1,2,0:T(8,128)(2,1)}, bf16[4,256,52,128]{3,1,2,0:T(8,128)(2,1)}, u32[]{:S(2)}, u32[]{:S(2)}) collective-permute-start(bf16[4,256,52,128]{3,1,2,0:T(8,128)(2,1)} %get-tuple-element.351), channel_id=1, source_target_pairs={{0,1},{1,2},{2,3},{3,4},{4,5},{5,6},{6,7},{7,0},{8,9},{9,10},{10,1... | collective-permute-start | bytes 40894472 | tf_op jit(solution)/shard_map/while/body/eval_jaxpr/ppermute | solution.py:84
  2980.0 233.9 %collective-permute-start = (bf16[4,256,52,128]{3,1,2,0:T(8,128)(2,1)}, bf16[4,256,52,128]{3,1,2,0:T(8,128)(2,1)}, u32[]{:S(2)}, u32[]{:S(2)}) collective-permute-start(bf16[4,256,52,128]{3,1,2,0:T(8,128)(2,1)} %get-tuple-element.350), channel_id=1, source_target_pairs={{0,1},{1,2},{2,3},{3,4},{4,5},{5,6},{6,7},{7,0},{8,9},{9,10},{10,1... | collective-permute-start | bytes 40894472 | tf_op jit(solution)/shard_map/while/body/eval_jaxpr/ppermute | solution.py:83
  2980.0 380.0 %collective-permute-start.1 = (bf16[4,256,52,128]{3,1,2,0:T(8,128)(2,1)}, bf16[4,256,52,128]{3,1,2,0:T(8,128)(2,1)}, u32[]{:S(2)}, u32[]{:S(2)}) collective-permute-start(bf16[4,256,52,128]{3,1,2,0:T(8,128)(2,1)} %get-tuple-element.351), channel_id=1, source_target_pairs={{0,1},{1,2},{2,3},{3,4},{4,5},{5,6},{6,7},{7,0},{8,9},{9,10},{10,1... | collective-permute-start | bytes 40894472 | tf_op jit(solution)/shard_map/while/body/eval_jaxpr/ppermute | solution.py:84
  3631.6 114.5 %copy-start.3 = (f32[52]{0:T(128)}, f32[52]{0:T(128)S(1)}, u32[]{:S(2)}) copy-start(f32[52]{0:T(128)S(1)} %pmax.7) | copy-start | bytes 628
where the time goes:
time: 3760 us; the launch traced here: 3750 us
  waiting for transfers between devices  2390 us (64%)
  matrix products  479 us (13%)
  local copies, waits for them, and re-layouts  343 us (9%)
  other arithmetic  230 us (6%)
  starting transfers between devices  190 us (5%)
  blocking collectives  116 us (3%)
    ppermute x7, waiting for transfers between devices, step(): k_blk = lax.ppermute(k_blk, 'cp', shift_pairs)  1360 us
    ppermute x7, waiting for transfers between devices, step(): v_blk = lax.ppermute(v_blk, 'cp', shift_pairs)  1020 us
    while x14, local copies, waits for them, and re-layouts  145 us
    pmax x1, blocking collectives, device_body(): head_max = lax.pmax(head_max, ('dp', 'cp'))  116 us
    convert_element_type x1, other arithmetic, clip_weights(): (w_k.astype(jnp.float32) * col_factor).astype(jnp.bfloat16)  114 us
    dot_general x1, matrix products, project_heads(): jnp.dot(hidden, w_k, preferred_element_type=jnp.float32).reshape(head_shape)  110 us
    dot_general x1, matrix products, project_heads(): jnp.dot(hidden, w_q, preferred_element_type=jnp.float32).reshape(head_shape)  110 us
    dot_general x1, matrix products, project_heads(): jnp.dot(hidden, w_v, preferred_element_type=jnp.float32)  101 us
  transfers between devices with their start and end apart: 14, of which 14 were waited for; matrix products, arithmetic and copies ran while one was open for 0% of the time, Pallas kernels for 0%

commit v1 on v0

v1 whole, which is shorter than its diff:
```python
import functools

import jax
import jax.numpy as jnp
from jax import lax
from jax.experimental import pallas as pl
from jax.experimental.pallas import tpu as pltpu
from jax.sharding import PartitionSpec as P


HEAD_DIM = 128
TAU_CLIP = 100.0
ROPE_THETA = 50000.0
TILE_N = 256
LOG2_E = 1.4426950408889634
VMEM_LIMIT = 62 * 1024 * 1024


def rope_tables(pos_ids):
    half_dim = HEAD_DIM // 2
    inv_freq = jnp.float32(ROPE_THETA) ** (-jnp.arange(half_dim, dtype=jnp.float32) * (2.0 / HEAD_DIM))
    angle = pos_ids.astype(jnp.float32)[:, None] * inv_freq[None, :]
    cos_t, sin_t = jnp.cos(angle), jnp.sin(angle)
    return jnp.concatenate([cos_t, cos_t], axis=-1), jnp.concatenate([-sin_t, sin_t], axis=-1)


def proj_kernel(n_chunks, n_alias, idx_ref, *refs):
    pieces = refs[: 2 * n_chunks]
    cos_ref, sin_ref, wq_ref, wk_ref, wv_ref = refs[2 * n_chunks : 2 * n_chunks + 5]
    q_ref, k_ref, v_ref, x_scr, sems = refs[2 * n_chunks + 5 + n_alias :]
    tile, chunk = pl.program_id(0), pl.program_id(1)
    rows = pieces[0].shape[0]
    core = idx_ref[0]

    def piece_copy(c, side):
        row0 = (core if side == 0 else 1 - core) * rows
        return pltpu.make_async_copy(
            pieces[2 * c + side], x_scr.at[c, pl.ds(pl.multiple_of(row0, rows), rows)], sems.at[c, side]
        )

    @pl.when(jnp.logical_and(tile == 0, chunk == 0))
    def _():
        for c in range(n_chunks):
            for side in range(2):
                piece_copy(c, side).start()

    for c in range(n_chunks):

        @pl.when(jnp.logical_and(tile == 0, chunk == c))
        def _():
            for side in range(2):
                piece_copy(c, side).wait()

    x = x_scr[chunk]
    cos_t, sin_t = cos_ref[0], sin_ref[0]
    for w_ref, o_ref in ((wq_ref, q_ref), (wk_ref, k_ref)):
        acc = jnp.dot(x, w_ref[...], preferred_element_type=jnp.float32)
        for h in range(TILE_N // HEAD_DIM):
            cols = slice(h * HEAD_DIM, (h + 1) * HEAD_DIM)
            t = acc[:, cols]
            o_ref[0, :, cols] = (t * cos_t + pltpu.roll(t, HEAD_DIM // 2, 1) * sin_t).astype(o_ref.dtype)
    v_ref[0] = jnp.dot(x, wv_ref[...], preferred_element_type=jnp.float32).astype(v_ref.dtype)


def project(idx, pieces, cos_t, sin_t, w_q, w_k, w_v, into, tile0, n_tiles):
    n_chunks = len(pieces) // 2
    rows, depth = pieces[0].shape
    total_chunks = cos_t.shape[0]
    half_cols = w_q.shape[1] // 2
    half_tiles = half_cols // TILE_N
    table_spec = pl.BlockSpec((1, 2 * rows, HEAD_DIM), lambda n, c, idx: (idx[1 + c], 0, 0))
    w_spec = pl.BlockSpec((depth, TILE_N), lambda n, c, idx: (0, idx[0] * half_tiles + tile0 + n))
    o_spec = pl.BlockSpec((1, 2 * rows, TILE_N), lambda n, c, idx: (idx[1 + c], 0, tile0 + n))
    any_spec = pl.BlockSpec(memory_space=pl.ANY)
    n_alias = 0 if into is None else 3
    o_shape = jax.ShapeDtypeStruct((total_chunks, 2 * rows, half_cols), jnp.bfloat16)
    flops = 2 * 3 * n_chunks * 2 * rows * depth * n_tiles * TILE_N
    first_alias = 1 + 2 * n_chunks + 5
    return pl.pallas_call(
        functools.partial(proj_kernel, n_chunks, n_alias),
        grid_spec=pltpu.PrefetchScalarGridSpec(
            num_scalar_prefetch=1,
            grid=(n_tiles, n_chunks),
            in_specs=[any_spec] * (2 * n_chunks) + [table_spec] * 2 + [w_spec] * 3 + [any_spec] * n_alias,
            out_specs=[o_spec] * 3,
            scratch_shapes=[
                pltpu.VMEM((n_chunks, 2 * rows, depth), jnp.bfloat16),
                pltpu.SemaphoreType.DMA((n_chunks, 2)),
            ],
        ),
        out_shape=[o_shape] * 3,
        input_output_aliases={first_alias + i: i for i in range(n_alias)},
        compiler_params=pltpu.CompilerParams(
            dimension_semantics=("arbitrary", "arbitrary"), vmem_limit_bytes=VMEM_LIMIT
        ),
        cost_estimate=pl.CostEstimate(
            flops=flops, bytes_accessed=2 * 3 * depth * n_tiles * TILE_N + 2 * n_chunks * rows * depth * 2, transcendentals=0
        ),
    )(idx, *pieces, cos_t, sin_t, w_q, w_k, w_v, *(into or ()))


def attn_kernel(blk, q_ref, k_ref, v_ref, o_ref, m_ref, s_scr):
    n_chunks, rows, _ = q_ref.shape
    per_chunk = rows // blk
    n_blocks = n_chunks * per_chunk
    scale = HEAD_DIM ** -0.5

    def rows_of(ref, i):
        r0 = (i % per_chunk) * blk
        return ref[i // per_chunk, r0 : r0 + blk, :]

    causal = lax.broadcasted_iota(jnp.int32, (blk, blk), 0) >= lax.broadcasted_iota(jnp.int32, (blk, blk), 1)
    head_max = None
    for i in range(n_blocks):
        q = rows_of(q_ref, i)
        lane_max = None
        for j in range(i + 1):
            s = lax.dot_general(q, rows_of(k_ref, j), (((1,), (1,)), ((), ())), preferred_element_type=jnp.float32)
            if j == i:
                s = jnp.where(causal, s, -jnp.inf)
            s_scr[i % 2, :, j * blk : (j + 1) * blk] = s
            for c in range(blk // HEAD_DIM):
                part = s[:, c * HEAD_DIM : (c + 1) * HEAD_DIM]
                lane_max = part if lane_max is None else jnp.maximum(lane_max, part)
        row_max = jnp.max(lane_max, axis=-1, keepdims=True)
        blk_max = jnp.max(lane_max.reshape(blk // 8, 8, HEAD_DIM), axis=0)
        head_max = blk_max if head_max is None else jnp.maximum(head_max, blk_max)
        lane_sum, acc = None, None
        for j in range(i + 1):
            p = jnp.exp2((s_scr[i % 2, :, j * blk : (j + 1) * blk] - row_max) * (scale * LOG2_E))
            for c in range(blk // HEAD_DIM):
                part = p[:, c * HEAD_DIM : (c + 1) * HEAD_DIM]
                lane_sum = part if lane_sum is None else lane_sum + part
            pv = jnp.dot(p.astype(jnp.bfloat16), rows_of(v_ref, j), preferred_element_type=jnp.float32)
            acc = pv if acc is None else acc + pv
        row_sum = jnp.sum(lane_sum, axis=-1, keepdims=True)
        r0 = (i % per_chunk) * blk
        o_ref[i // per_chunk, r0 : r0 + blk, :] = (acc / row_sum).astype(o_ref.dtype)
    m_ref[...] = head_max * scale


def attend(q, k, v, head0, n_heads):
    n_chunks, rows, _ = q.shape
    blk = min(256, rows)
    in_spec = pl.BlockSpec((n_chunks, rows, HEAD_DIM), lambda h: (0, 0, head0 + h))
    o_spec = pl.BlockSpec((n_chunks, rows, HEAD_DIM), lambda h: (0, 0, h))
    seq = n_chunks * rows
    return pl.pallas_call(
        functools.partial(attn_kernel, blk),
        grid=(n_heads,),
        in_specs=[in_spec] * 3,
        out_specs=[o_spec, pl.BlockSpec((8, HEAD_DIM), lambda h: (h, 0))],
        out_shape=[
            jax.ShapeDtypeStruct((n_chunks, rows, n_heads * HEAD_DIM), jnp.bfloat16),
            jax.ShapeDtypeStruct((8 * n_heads, HEAD_DIM), jnp.float32),
        ],
        scratch_shapes=[pltpu.VMEM((2, blk, seq), jnp.float32)],
        compiler_params=pltpu.CompilerParams(dimension_semantics=("arbitrary",), vmem_limit_bytes=VMEM_LIMIT),
        cost_estimate=pl.CostEstimate(
            flops=8 * seq * seq * HEAD_DIM * n_heads // 2,
            bytes_accessed=8 * seq * HEAD_DIM * n_heads,
            transcendentals=seq * seq * n_heads // 2,
        ),
    )(q, k, v)


def out_kernel(n_chunks, col_offs, n_alias, idx_ref, *refs):
    n_groups = len(col_offs)
    n_pieces = n_chunks * 2 * n_groups
    pieces = refs[:n_pieces]
    wo_ref, fac_ref, wc_ref = refs[n_pieces : n_pieces + 3]
    o_hbm, c_ref, a_scr, o_scr, a_sems, o_sems = refs[n_pieces + 3 + n_alias :]
    tile, n_tiles = pl.program_id(0), pl.num_programs(0)
    core = idx_ref[0]
    rows = pieces[0].shape[0]
    half_cols = a_scr.shape[1] // 2

    def piece_copies():
        copies = []
        for c in range(n_chunks):
            for side in range(2):
                for g in range(n_groups):
                    n = (c * 2 + side) * n_groups + g
                    col0 = (core if side == 0 else 1 - core) * half_cols + col_offs[g]
                    width = pieces[n].shape[1]
                    copies.append(
                        pltpu.make_async_copy(
                            pieces[n],
                            a_scr.at[pl.ds(c * rows, rows), pl.ds(pl.multiple_of(col0, HEAD_DIM), width)],
                            a_sems.at[n],
                        )
                    )
        return copies

    def out_copies(slot, at_tile):
        return [
            pltpu.make_async_copy(
                o_scr.at[slot, pl.ds(c * rows, rows)],
                o_hbm.at[idx_ref[1 + c], :, pl.ds(pl.multiple_of(at_tile * TILE_N, TILE_N), TILE_N)],
                o_sems.at[slot, c],
            )
            for c in range(n_chunks)
        ]

    @pl.when(tile == 0)
    def _():
        for copy in piece_copies():
            copy.start()
        for copy in piece_copies():
            copy.wait()

    slot = lax.rem(tile, 2)

    @pl.when(tile >= 2)
    def _():
        for copy in out_copies(slot, tile - 2):
            copy.wait()

    o_scr[slot] = jnp.dot(a_scr[...], wo_ref[...], preferred_element_type=jnp.float32).astype(o_scr.dtype)
    c_ref[...] = (wc_ref[...].astype(jnp.float32) * fac_ref[...]).astype(c_ref.dtype)
    for copy in out_copies(slot, tile):
        copy.start()

    @pl.when(tile == n_tiles - 1)
    def _():
        for copy in out_copies(1 - slot, tile - 1):
            copy.wait()
        for copy in out_copies(slot, tile):
            copy.wait()


def out_project(idx, pieces, col_offs, w_o, factor, w_clip, into, out_shape):
    n_groups = len(col_offs)
    n_chunks = len(pieces) // (2 * n_groups)
    rows = pieces[0].shape[0]
    depth, width = w_o.shape
    n_tiles = width // TILE_N
    any_spec = pl.BlockSpec(memory_space=pl.ANY)
    tile_spec = pl.BlockSpec((depth, TILE_N), lambda n, idx: (0, n))
    n_alias = 0 if into is None else 1
    alias_at = 1 + len(pieces) + 3
    return pl.pallas_call(
        functools.partial(out_kernel, n_chunks, col_offs, n_alias),
        grid_spec=pltpu.PrefetchScalarGridSpec(
            num_scalar_prefetch=1,
            grid=(n_tiles,),
            in_specs=[any_spec] * len(pieces)
            + [tile_spec, pl.BlockSpec((1, TILE_N), lambda n, idx: (0, n)), tile_spec]
            + [any_spec] * n_alias,
            out_specs=[any_spec, tile_spec],
            scratch_shapes=[
                pltpu.VMEM((n_chunks * rows, depth), jnp.bfloat16),
                pltpu.VMEM((2, n_chunks * rows, TILE_N), jnp.bfloat16),
                pltpu.SemaphoreType.DMA((len(pieces),)),
                pltpu.SemaphoreType.DMA((2, n_chunks)),
            ],
        ),
        out_shape=[jax.ShapeDtypeStruct(out_shape, jnp.bfloat16), jax.ShapeDtypeStruct(w_clip.shape, jnp.bfloat16)],
        input_output_aliases={alias_at: 0} if n_alias else {},
        compiler_params=pltpu.CompilerParams(dimension_semantics=("arbitrary",), vmem_limit_bytes=VMEM_LIMIT),
        cost_estimate=pl.CostEstimate(
            flops=2 * n_chunks * rows * depth * width, bytes_accessed=2 * 3 * depth * width, transcendentals=0
        ),
    )(idx, *pieces, w_o, factor, w_clip, *([into] if n_alias else []))


def solution(mesh):
    cp_size = mesh.shape["cp"]
    n_chips = cp_size // 2

    def permute(x, flip):
        return lax.ppermute(x, "cp", [(src, src ^ flip) for src in range(cp_size)])

    def device_body(hidden, pos_ids, w_q, w_k, w_v, w_o):
        cp_rank = lax.axis_index("cp")
        core, chip = cp_rank % 2, cp_rank // 2
        n_heads = w_q.shape[1] // HEAD_DIM
        half_heads = n_heads // 2
        half_tiles = half_heads * HEAD_DIM // TILE_N
        tiles_a = (half_tiles + 1) // 2
        heads_per_tile = TILE_N // HEAD_DIM
        groups = [(0, tiles_a), (tiles_a, half_tiles - tiles_a)]
        col_offs = tuple(t0 * TILE_N for t0, _ in groups)

        def index(*offsets):
            return jnp.stack([core] + [chip ^ d for d in offsets]).astype(jnp.int32)

        same, other = {}, {}
        for d in range(n_chips):
            row = lax.dynamic_index_in_dim(hidden, chip ^ d, 0, keepdims=False)
            same[d] = permute(row, 2 * d) if d else row
            other[d] = permute(same[d], 1)

        all_pos = lax.all_gather(pos_ids, "cp", tiled=True)
        cos_t, sin_t = (t.reshape(n_chips, -1, HEAD_DIM) for t in rope_tables(all_pos))

        def fill(qkv, offsets, tile0, n_tiles):
            pieces = [piece for d in offsets for piece in (same[d], other[d])]
            return project(index(*offsets), pieces, cos_t, sin_t, w_q, w_k, w_v, qkv, tile0, n_tiles)

        rest = tuple(range(1, n_chips))
        qkv = fill(None, (0,), 0, tiles_a)
        qkv = fill(qkv, (0,), tiles_a, half_tiles - tiles_a)
        for d in rest:
            qkv = fill(qkv, (d,), *groups[0])

        sent, maxes = [], []
        for g, (tile0, n_tiles) in enumerate(groups):
            if g == 1:
                qkv = fill(qkv, rest, tile0, n_tiles)
            vals, row_max = attend(*qkv, tile0 * heads_per_tile, n_tiles * heads_per_tile)
            maxes.append(jnp.max(row_max.reshape(n_tiles * heads_per_tile, -1), axis=1))
            vals = vals.reshape(cp_size, -1, vals.shape[-1])
            got = {}
            for d in range(n_chips):
                for side in range(2):
                    piece = lax.dynamic_index_in_dim(vals, cp_rank ^ (2 * d + side), 0, keepdims=False)
                    got[d, side] = permute(piece, 2 * d + side) if d or side else piece
            sent.append(got)

        local_max = jnp.concatenate(maxes)
        spread = jnp.full((2, half_heads), -jnp.inf, jnp.float32)
        spread = lax.dynamic_update_slice(spread, local_max[None], (core, 0)).reshape(n_heads)
        head_max = lax.pmax(spread, ("dp", "cp"))
        factor = jnp.where(head_max > TAU_CLIP, jnp.sqrt(TAU_CLIP / head_max), 1.0)
        factor = jnp.repeat(factor, HEAD_DIM)[None, :]

        def out_rows(offsets, w_clip, into):
            pieces = [sent[g][d, side] for d in offsets for side in range(2) for g in range(len(groups))]
            return out_project(index(*offsets), pieces, col_offs, w_o, factor, w_clip, into, hidden.shape)

        attn_out, w_q_new = out_rows((0,), w_q, None)
        attn_out, w_k_new = out_rows(rest, w_k, attn_out)
        return attn_out, head_max, w_q_new, w_k_new

    return jax.shard_map(
        device_body,
        mesh=mesh,
        in_specs=(P("dp", "cp", None), P("cp"), P(None, None), P(None, None), P(None, None), P(None, None)),
        out_specs=(P("dp", "cp", None), P(None), P(None, None), P(None, None)),
        check_vma=False,
    )
```

time: 3760 us -> 1010 us (0.27)
  waiting for transfers between devices: 2390 us -> 61.2 us
  Pallas kernels: 0 us -> 697 us
  matrix products: 479 us -> 0 us
  local copies, waits for them, and re-layouts: 343 us -> 22.5 us
  other arithmetic: 230 us -> 9.28 us
  starting transfers between devices: 190 us -> 19.3 us
  blocking collectives: 116 us -> 195 us
    ppermute x14 -> x21, waiting for transfers between devices: 2390 us -> 61.2 us  [permute(): return lax.ppermute(x, 'cp', [(src, src ^ flip) for src in range(cp_size)])]
    pallas_call x0 -> x10, Pallas kernels: none -> 697 us  [the longest x6 355 us: project(): pl.pallas_call(functools.partial(proj_kernel, n_chunks, n_alias), grid_sp...]
    dot_general x6 -> x0, matrix products: 479 us -> none  [the longest x1 110 us: project_heads(): jnp.dot(hidden, w_k, preferred_element_type=jnp.float32).reshape(head_shape)]
    while x17 -> x0, local copies, waits for them, and re-layouts: 213 us -> none
    ppermute x14 -> x21, starting transfers between devices: 190 us -> 19.3 us  [permute(): return lax.ppermute(x, 'cp', [(src, src ^ flip) for src in range(cp_size)])]
    all_gather x0 -> x1, blocking collectives: none -> 151 us  [device_body(): all_pos = lax.all_gather(pos_ids, 'cp', tiled=True)]
    convert_element_type x2 -> x0, other arithmetic: 126 us -> none  [the longest x1 114 us: clip_weights(): (w_k.astype(jnp.float32) * col_factor).astype(jnp.bfloat16)]
    unnamed x12 -> x22, local copies, waits for them, and re-layouts: 76.6 us -> 2.59 us
  transfers between devices with their start and end apart: 14 -> 21, of which waited for: 14 -> 3; matrix products, arithmetic and copies ran while one was open for 0% -> 2% of each run, Pallas kernels for 0% -> 30%
where the time goes in v1:
time: 1010 us
  Pallas kernels  697 us (69%)
  blocking collectives  195 us (19%)
  waiting for transfers between devices  61.2 us (6%)
  local copies, waits for them, and re-layouts  22.5 us (2%)
  starting transfers between devices  19.3 us (2%)
    pallas_call x6, Pallas kernels, project(): pl.pallas_call(functools.partial(proj_kernel, n_chunks, n_alias), grid_sp...  355 us
    pallas_call x2, Pallas kernels, out_project(): pl.pallas_call(functools.partial(out_kernel, n_chunks, col_offs, n_alias)...  219 us
    all_gather x1, blocking collectives, device_body(): all_pos = lax.all_gather(pos_ids, 'cp', tiled=True)  151 us
    pallas_call x2, Pallas kernels, attend(): pl.pallas_call(functools.partial(attn_kernel, blk), grid=(n_heads,), in_s...  123 us
    ppermute x21, waiting for transfers between devices, permute(): return lax.ppermute(x, 'cp', [(src, src ^ flip) for src in range(cp_size)])  61.2 us
    pmax x1, blocking collectives, device_body(): head_max = lax.pmax(spread, ('dp', 'cp'))  44.3 us
  transfers between devices with their start and end apart: 21, of which 3 were waited for; matrix products, arithmetic and copies ran while one was open for 2% of the time, Pallas kernels for 30%

profile of v1, /device:TPU:0, one launch (start us, length us, event | category | flops | bytes accessed | tf_op | source)
XLA Modules:
  0.0 1005.8 jit_solution(7910921241327438779)
XLA Ops:
  0.7 9.2 dynamic-slice_bitcast_fusion
  9.9 3.2 collective-permute-start.2
  14.6 150.9 %all-gather = s32[8,1,256]{2,1,0:T(1,128)S(1)} all-gather(s32[1,1,256]{2,1,0:T(1,128)S(1)} %bitcast.60), channel_id=1, replica_groups=mesh['dp'=2,'cp'=8] {'cp'}, dimensions={0}, use_global_device_ids=true | all-gather | bytes 9216 | tf_op jit(solution)/shard_map/all_gather | solution.py:294
  168.6 3.7 fusion
  172.4 2.0 pad_maximum_fusion
  175.3 50.2 %shard_map.93 = (bf16[4,512,3328]{2,1,0:T(8,128)(2,1)}, bf16[4,512,3328]{2,1,0:T(8,128)(2,1)}, bf16[4,512,3328]{2,1,0:T(8,128)(2,1)}) custom-call(s32[2]{0:T(128)} %pad_add_fusion.4.idx_ref, bf16[256,6656]{1,0:T(8,128)(2,1)} %copy-done, bf16[256,6656]{1,0:T(8,128)(2,1)} %collective-permute-done.6.refs_1_, f32[4,512,128]{2,1,0:T(8,128)} %get-tuple-element.79.refs_2_.refs_6_, ...), custom_call_target="tpu_custom_call" | custom-call | flops 36641439744 | bytes 78381056 | tf_op jit(solution)/shard_map/pallas_call | solution.py:79
  225.5 44.3 %shard_map.94 = (bf16[4,512,3328]{2,1,0:T(8,128)(2,1)}, bf16[4,512,3328]{2,1,0:T(8,128)(2,1)}, bf16[4,512,3328]{2,1,0:T(8,128)(2,1)}) custom-call(s32[2]{0:T(128)} %pad_add_fusion.4.idx_ref, bf16[256,6656]{1,0:T(8,128)(2,1)} %copy-done, ...), custom_call_target="tpu_custom_call", output_to_operand_aliasing={{0}: (8, {}), {1}: (9, {}), {2}: (10, {})} | custom-call | flops 31406948352 | bytes 68157440 | tf_op jit(solution)/shard_map/pallas_call | solution.py:79
  269.8 50.0 %shard_map.95 = (bf16[4,512,3328]{2,1,0:T(8,128)(2,1)}, bf16[4,512,3328]{2,1,0:T(8,128)(2,1)}, bf16[4,512,3328]{2,1,0:T(8,128)(2,1)}) custom-call(s32[2]{0:T(128)} %pad_add_fusion.3.idx_ref, bf16[256,6656]{1,0:T(8,128)(2,1)} %collective-permute-done.4.refs_0_, ...), custom_call_target="tpu_custom_call", output_to_operand_aliasing={{0}: (8, {}), {1}: (9, {}), {2}: (10, {})} | custom-call | flops 36641439744 | bytes 78381056 | tf_op jit(solution)/shard_map/pallas_call | solution.py:79
  319.8 50.5 %shard_map.96 = (bf16[4,512,3328]{2,1,0:T(8,128)(2,1)}, bf16[4,512,3328]{2,1,0:T(8,128)(2,1)}, bf16[4,512,3328]{2,1,0:T(8,128)(2,1)}) custom-call(s32[2]{0:T(128)} %pad_add_fusion.2.idx_ref, bf16[256,6656]{1,0:T(8,128)(2,1)} %collective-permute-done.2.refs_0_.refs_2_, ...), custom_call_target="tpu_custom_call", output_to_operand_aliasing={{0}: (8, {}), {1}: (9, {}), {2}: (10, {})} | custom-call | flops 36641439744 | bytes 78381056 | tf_op jit(solution)/shard_map/pallas_call | solution.py:79
  370.3 49.9 %shard_map.97 = (bf16[4,512,3328]{2,1,0:T(8,128)(2,1)}, bf16[4,512,3328]{2,1,0:T(8,128)(2,1)}, bf16[4,512,3328]{2,1,0:T(8,128)(2,1)}) custom-call(s32[2]{0:T(128)} %pad_add_fusion.1.idx_ref, bf16[256,6656]{1,0:T(8,128)(2,1)} %collective-permute-done.refs_0_.refs_4_, ...), custom_call_target="tpu_custom_call", output_to_operand_aliasing={{0}: (8, {}), {1}: (9, {}), {2}: (10, {})} | custom-call | flops 36641439744 | bytes 78381056 | tf_op jit(solution)/shard_map/pallas_call | solution.py:79
  420.2 65.9 %shard_map.98 = (bf16[4,512,1792]{2,1,0:T(8,128)(2,1)}, f32[112,128]{1,0:T(8,128)}) custom-call(bf16[4,512,3328]{2,1,0:T(8,128)(2,1)} %get-tuple-element.42.q_ref.refs_11_, bf16[4,512,3328]{2,1,0:T(8,128)(2,1)} %get-tuple-element.43.k_ref.refs_12_, bf16[4,512,3328]{2,1,0:T(8,128)(2,1)} %get-tuple-element.44.v_ref.refs_13_), custom_call_target="tpu_custom_call" | custom-call | flops 30064771072 | bytes 29360128 | tf_op jit(solution)/shard_map/pallas_call | solution.py:148
  486.2 110.4 %shard_map.99 = (bf16[4,512,3328]{2,1,0:T(8,128)(2,1)}, bf16[4,512,3328]{2,1,0:T(8,128)(2,1)}, bf16[4,512,3328]{2,1,0:T(8,128)(2,1)}) custom-call(s32[4]{0:T(128)} %pad_add_fusion.idx_ref, bf16[256,6656]{1,0:T(8,128)(2,1)} %collective-permute-done.4.refs_0_, ...), custom_call_target="tpu_custom_call", output_to_operand_aliasing={{0}: (12, {}), {1}: (13, {}), {2}: (14, {})} | custom-call | flops 94220845056 | bytes 81788928 | tf_op jit(solution)/shard_map/pallas_call | solution.py:79
  596.6 56.9 %shard_map.100 = (bf16[4,512,1536]{2,1,0:T(8,128)(2,1)}, f32[96,128]{1,0:T(8,128)}) custom-call(bf16[4,512,3328]{2,1,0:T(8,128)(2,1)} %get-tuple-element.46.q_ref, bf16[4,512,3328]{2,1,0:T(8,128)(2,1)} %get-tuple-element.47.k_ref, bf16[4,512,3328]{2,1,0:T(8,128)(2,1)} %get-tuple-element.48.v_ref), custom_call_target="tpu_custom_call" | custom-call | flops 25769803776 | bytes 25165824 | tf_op jit(solution)/shard_map/pallas_call | solution.py:148
  653.5 4.8 dynamic-slice_bitcast_fusion.12
  658.4 1.8 collective-permute-start.18
  662.4 5.6 dynamic-slice_bitcast_fusion.4
  669.7 8.9 collective-permute-done.18.refs_11_
  678.5 1.6 collective-permute-start.12
  680.1 16.6 %collective-permute-done.16.refs_9_ = bf16[256,1536]{1,0:T(8,128)(2,1)S(1)} collective-permute-done((bf16[256,1536]{1,0:T(8,128)(2,1)S(1)}, bf16[256,1536]{1,0:T(8,128)(2,1)S(1)}, u32[]{:S(2)}, u32[]{:S(2)}) %collective-permute-start.16) | collective-permute-done | bytes 786464 | tf_op jit(solution)/shard_map/ppermute | solution.py:272
  696.8 35.7 %collective-permute-done.14.refs_7_ = bf16[256,1536]{1,0:T(8,128)(2,1)S(1)} collective-permute-done((bf16[256,1536]{1,0:T(8,128)(2,1)S(1)}, bf16[256,1536]{1,0:T(8,128)(2,1)S(1)}, u32[]{:S(2)}, u32[]{:S(2)}) %collective-permute-start.14) | collective-permute-done | bytes 786464 | tf_op jit(solution)/shard_map/ppermute | solution.py:272
  734.8 44.3 %pmax.7 = f32[52]{0:T(128)S(1)} all-reduce(f32[52]{0:T(128)S(1)} %reshape.73), channel_id=1, replica_groups=mesh['dp'=2,'cp'=8] {'dp','cp'}, use_global_device_ids=true, to_apply=%region_4.5 | all-reduce | flops 52 | bytes 416 | tf_op jit(solution)/shard_map/pmax | solution.py:324
  779.8 3.3 collective-permute-start.15
  786.6 102.9 %shard_map.101 = (bf16[4,256,6656]{2,1,0:T(8,128)(2,1)}, bf16[6656,6656]{1,0:T(8,128)(2,1)}) custom-call(s32[2]{0:T(128)} %pad_add_fusion.4.idx_ref, bf16[256,1792]{1,0:T(8,128)(2,1)} %get-tuple-element.61.refs_0_, bf16[256,1536]{1,0:T(8,128)(2,1)} %get-tuple-element.69.refs_1_, bf16[256,1792]{1,0:T(8,128)(2,1)} %copy-done.1, bf16[256,1536]{1,0:T(8,128)(2,1)} %copy-done.2, ...), custom_call_target="tpu_custom_call" | custom-call | flops 22682796032 | bytes 265814016 | tf_op jit(solution)/shard_map/pallas_call | solution.py:242
  889.6 116.0 %shard_map.102 = (bf16[4,256,6656]{2,1,0:T(8,128)(2,1)}, bf16[6656,6656]{1,0:T(8,128)(2,1)}) custom-call(s32[4]{0:T(128)} %pad_add_fusion.idx_ref, bf16[256,1792]{1,0:T(8,128)(2,1)} %collective-permute-done.7.refs_0_, bf16[256,1536]{1,0:T(8,128)(2,1)} %collective-permute-done.8.refs_1_, ...), custom_call_target="tpu_custom_call", output_to_operand_aliasing={{0}: (16, {})} | custom-call | flops 68048388096 | bytes 265814016 | tf_op jit(solution)/shard_map/pallas_call | solution.py:242
  (76 shorter events, 15.9 us)
Async XLA Ops:
  9.9 164.5 %collective-permute-start.2 = (bf16[256,6656]{1,0:T(8,128)(2,1)}, bf16[256,6656]{1,0:T(8,128)(2,1)}, u32[]{:S(2)}, u32[]{:S(2)}) collective-permute-start(bf16[256,6656]{1,0:T(8,128)(2,1)} %get-tuple-element.57), channel_id=1, source_target_pairs={{0,4},{1,5},{2,6},{3,7},{4,0},{5,1},{6,2},{7,3},{8,12},{9,13},{10,... | collective-permute-start | bytes 10223624 | tf_op jit(solution)/shard_map/ppermute | solution.py:272
  13.1 161.6 %collective-permute-start = (bf16[256,6656]{1,0:T(8,128)(2,1)}, bf16[256,6656]{1,0:T(8,128)(2,1)}, u32[]{:S(2)}, u32[]{:S(2)}) collective-permute-start(bf16[256,6656]{1,0:T(8,128)(2,1)} %get-tuple-element.58), channel_id=1, source_target_pairs={{0,6},{1,7},{2,4},{3,5},{4,2},{5,3},{6,0},{7,1},{8,14},{9,15},{10,... | collective-permute-start | bytes 10223624 | tf_op jit(solution)/shard_map/ppermute | solution.py:272
  14.6 160.4 %collective-permute-start.4 = (bf16[256,6656]{1,0:T(8,128)(2,1)}, bf16[256,6656]{1,0:T(8,128)(2,1)}, u32[]{:S(2)}, u32[]{:S(2)}) collective-permute-start(bf16[256,6656]{1,0:T(8,128)(2,1)} %get-tuple-element.59), channel_id=1, source_target_pairs={{0,2},{1,3},{2,0},{3,1},{4,6},{5,7},{6,4},{7,5},{8,10},{9,11},{10,... | collective-permute-start | bytes 10223624 | tf_op jit(solution)/shard_map/ppermute | solution.py:272
  14.6 160.6 %collective-permute-start.6 = (bf16[256,6656]{1,0:T(8,128)(2,1)S(1)}, bf16[256,6656]{1,0:T(8,128)(2,1)}, u32[]{:S(2)}, u32[]{:S(2)}) collective-permute-start(bf16[256,6656]{1,0:T(8,128)(2,1)S(1)} %get-tuple-element.56.refs_0_), channel_id=1, source_target_pairs={{0,1},{1,0},{2,3},{3,2},{4,5},{5,4},{6,7},{7,6},{8,9},{9,8},{10,11... | collective-permute-start | bytes 10223624 | tf_op jit(solution)/shard_map/ppermute | solution.py:272
  174.4 145.4 %collective-permute-start.3 = (bf16[256,6656]{1,0:T(8,128)(2,1)}, bf16[256,6656]{1,0:T(8,128)(2,1)}, u32[]{:S(2)}, u32[]{:S(2)}) collective-permute-start(bf16[256,6656]{1,0:T(8,128)(2,1)} %collective-permute-done.2.refs_0_.refs_2_), channel_id=1, source_target_pairs={{0,1},{1,0},{2,3},{3,2},{4,5},{5,4},{6,7},{7,6},{8,9},{9,8},{10,11... | collective-permute-start | bytes 10223624 | tf_op jit(solution)/shard_map/ppermute | solution.py:272
  174.7 195.6 %collective-permute-start.1 = (bf16[256,6656]{1,0:T(8,128)(2,1)}, bf16[256,6656]{1,0:T(8,128)(2,1)}, u32[]{:S(2)}, u32[]{:S(2)}) collective-permute-start(bf16[256,6656]{1,0:T(8,128)(2,1)} %collective-permute-done.refs_0_.refs_4_), channel_id=1, source_target_pairs={{0,1},{1,0},{2,3},{3,2},{4,5},{5,4},{6,7},{7,6},{8,9},{9,8},{10,11... | collective-permute-start | bytes 10223624 | tf_op jit(solution)/shard_map/ppermute | solution.py:272
  174.9 94.9 %collective-permute-start.5 = (bf16[256,6656]{1,0:T(8,128)(2,1)}, bf16[256,6656]{1,0:T(8,128)(2,1)}, u32[]{:S(2)}, u32[]{:S(2)}) collective-permute-start(bf16[256,6656]{1,0:T(8,128)(2,1)} %collective-permute-done.4.refs_0_), channel_id=1, source_target_pairs={{0,1},{1,0},{2,3},{3,2},{4,5},{5,4},{6,7},{7,6},{8,9},{9,8},{10,11... | collective-permute-start | bytes 10223624 | tf_op jit(solution)/shard_map/ppermute | solution.py:272
  653.5 80.4 %copy-start.3 = (f32[112,128]{1,0:T(8,128)S(1)}, f32[112,128]{1,0:T(8,128)}, u32[]{:S(2)}) copy-start(f32[112,128]{1,0:T(8,128)} %get-tuple-element.50) | copy-start | bytes 172036
  653.5 80.5 %copy-start.4 = (f32[96,128]{1,0:T(8,128)S(1)}, f32[96,128]{1,0:T(8,128)}, u32[]{:S(2)}) copy-start(f32[96,128]{1,0:T(8,128)} %get-tuple-element.51) | copy-start | bytes 147460
  658.4 10.4 %collective-permute-start.20 = (bf16[256,1536]{1,0:T(8,128)(2,1)S(1)}, bf16[256,1536]{1,0:T(8,128)(2,1)S(1)}, u32[]{:S(2)}, u32[]{:S(2)}) collective-permute-start(bf16[256,1536]{1,0:T(8,128)(2,1)S(1)} %get-tuple-element.68), channel_id=1, source_target_pairs={{0,1},{1,0},{2,3},{3,2},{4,5},{5,4},{6,7},{7,6},{8,9},{9,8},{10,11... | collective-permute-start | bytes 2359304 | tf_op jit(solution)/shard_map/ppermute | solution.py:272
  658.4 20.1 %collective-permute-start.18 = (bf16[256,1536]{1,0:T(8,128)(2,1)S(1)}, bf16[256,1536]{1,0:T(8,128)(2,1)S(1)}, u32[]{:S(2)}, u32[]{:S(2)}) collective-permute-start(bf16[256,1536]{1,0:T(8,128)(2,1)S(1)} %get-tuple-element.70), channel_id=1, source_target_pairs={{0,7},{1,6},{2,5},{3,4},{4,3},{5,2},{6,1},{7,0},{8,15},{9,14},{10,... | collective-permute-start | bytes 2359304 | tf_op jit(solution)/shard_map/ppermute | solution.py:272
  660.1 36.6 %collective-permute-start.16 = (bf16[256,1536]{1,0:T(8,128)(2,1)S(1)}, bf16[256,1536]{1,0:T(8,128)(2,1)S(1)}, u32[]{:S(2)}, u32[]{:S(2)}) collective-permute-start(bf16[256,1536]{1,0:T(8,128)(2,1)S(1)} %get-tuple-element.71), channel_id=1, source_target_pairs={{0,6},{1,7},{2,4},{3,5},{4,2},{5,3},{6,0},{7,1},{8,14},{9,15},{10,... | collective-permute-start | bytes 2359304 | tf_op jit(solution)/shard_map/ppermute | solution.py:272
  661.4 71.1 %collective-permute-start.14 = (bf16[256,1536]{1,0:T(8,128)(2,1)S(1)}, bf16[256,1536]{1,0:T(8,128)(2,1)S(1)}, u32[]{:S(2)}, u32[]{:S(2)}) collective-permute-start(bf16[256,1536]{1,0:T(8,128)(2,1)S(1)} %get-tuple-element.72), channel_id=1, source_target_pairs={{0,5},{1,4},{2,7},{3,6},{4,1},{5,0},{6,3},{7,2},{8,13},{9,12},{10,... | collective-permute-start | bytes 2359304 | tf_op jit(solution)/shard_map/ppermute | solution.py:272
  668.0 115.6 %collective-permute-start.19 = (bf16[256,1792]{1,0:T(8,128)(2,1)}, bf16[256,1792]{1,0:T(8,128)(2,1)S(1)}, u32[]{:S(2)}, u32[]{:S(2)}) collective-permute-start(bf16[256,1792]{1,0:T(8,128)(2,1)} %get-tuple-element.60), channel_id=1, source_target_pairs={{0,1},{1,0},{2,3},{3,2},{4,5},{5,4},{6,7},{7,6},{8,9},{9,8},{10,11... | collective-permute-start | bytes 2752520 | tf_op jit(solution)/shard_map/ppermute | solution.py:272
  668.8 116.3 %collective-permute-start.17 = (bf16[256,1792]{1,0:T(8,128)(2,1)S(1)}, bf16[256,1792]{1,0:T(8,128)(2,1)}, u32[]{:S(2)}, u32[]{:S(2)}) collective-permute-start(bf16[256,1792]{1,0:T(8,128)(2,1)S(1)} %get-tuple-element.62), channel_id=1, source_target_pairs={{0,7},{1,6},{2,5},{3,4},{4,3},{5,2},{6,1},{7,0},{8,15},{9,14},{10,... | collective-permute-start | bytes 2752520 | tf_op jit(solution)/shard_map/ppermute | solution.py:272
  678.5 101.3 %collective-permute-start.12 = (bf16[256,1536]{1,0:T(8,128)(2,1)}, bf16[256,1536]{1,0:T(8,128)(2,1)}, u32[]{:S(2)}, u32[]{:S(2)}) collective-permute-start(bf16[256,1536]{1,0:T(8,128)(2,1)} %get-tuple-element.73), channel_id=1, source_target_pairs={{0,4},{1,5},{2,6},{3,7},{4,0},{5,1},{6,2},{7,3},{8,12},{9,13},{10,... | collective-permute-start | bytes 2359304 | tf_op jit(solution)/shard_map/ppermute | solution.py:272
  696.8 86.3 %collective-permute-start.10 = (bf16[256,1536]{1,0:T(8,128)(2,1)}, bf16[256,1536]{1,0:T(8,128)(2,1)}, u32[]{:S(2)}, u32[]{:S(2)}) collective-permute-start(bf16[256,1536]{1,0:T(8,128)(2,1)} %get-tuple-element.74), channel_id=1, source_target_pairs={{0,3},{1,2},{2,1},{3,0},{4,7},{5,6},{6,5},{7,4},{8,11},{9,10},{10,... | collective-permute-start | bytes 2359304 | tf_op jit(solution)/shard_map/ppermute | solution.py:272
  733.4 49.7 %collective-permute-start.8 = (bf16[256,1536]{1,0:T(8,128)(2,1)}, bf16[256,1536]{1,0:T(8,128)(2,1)}, u32[]{:S(2)}, u32[]{:S(2)}) collective-permute-start(bf16[256,1536]{1,0:T(8,128)(2,1)} %get-tuple-element.75), channel_id=1, source_target_pairs={{0,2},{1,3},{2,0},{3,1},{4,6},{5,7},{6,4},{7,5},{8,10},{9,11},{10,... | collective-permute-start | bytes 2359304 | tf_op jit(solution)/shard_map/ppermute | solution.py:272
  779.1 110.4 %copy-start.9 = (f32[52]{0:T(128)}, f32[52]{0:T(128)S(1)}, u32[]{:S(2)}) copy-start(f32[52]{0:T(128)S(1)} %pmax.7) | copy-start | bytes 628
  779.8 109.7 %collective-permute-start.15 = (bf16[256,1792]{1,0:T(8,128)(2,1)}, bf16[256,1792]{1,0:T(8,128)(2,1)}, u32[]{:S(2)}, u32[]{:S(2)}) collective-permute-start(bf16[256,1792]{1,0:T(8,128)(2,1)} %get-tuple-element.63), channel_id=1, source_target_pairs={{0,6},{1,7},{2,4},{3,5},{4,2},{5,3},{6,0},{7,1},{8,14},{9,15},{10,... | collective-permute-start | bytes 2752520 | tf_op jit(solution)/shard_map/ppermute | solution.py:272
  783.1 106.4 %collective-permute-start.13 = (bf16[256,1792]{1,0:T(8,128)(2,1)}, bf16[256,1792]{1,0:T(8,128)(2,1)}, u32[]{:S(2)}, u32[]{:S(2)}) collective-permute-start(bf16[256,1792]{1,0:T(8,128)(2,1)} %get-tuple-element.64), channel_id=1, source_target_pairs={{0,5},{1,4},{2,7},{3,6},{4,1},{5,0},{6,3},{7,2},{8,13},{9,12},{10,... | collective-permute-start | bytes 2752520 | tf_op jit(solution)/shard_map/ppermute | solution.py:272
  783.1 106.4 %collective-permute-start.11 = (bf16[256,1792]{1,0:T(8,128)(2,1)}, bf16[256,1792]{1,0:T(8,128)(2,1)}, u32[]{:S(2)}, u32[]{:S(2)}) collective-permute-start(bf16[256,1792]{1,0:T(8,128)(2,1)} %get-tuple-element.65), channel_id=1, source_target_pairs={{0,4},{1,5},{2,6},{3,7},{4,0},{5,1},{6,2},{7,3},{8,12},{9,13},{10,... | collective-permute-start | bytes 2752520 | tf_op jit(solution)/shard_map/ppermute | solution.py:272
  783.6 105.9 %collective-permute-start.9 = (bf16[256,1792]{1,0:T(8,128)(2,1)}, bf16[256,1792]{1,0:T(8,128)(2,1)}, u32[]{:S(2)}, u32[]{:S(2)}) collective-permute-start(bf16[256,1792]{1,0:T(8,128)(2,1)} %get-tuple-element.66), channel_id=1, source_target_pairs={{0,3},{1,2},{2,1},{3,0},{4,7},{5,6},{6,5},{7,4},{8,11},{9,10},{10,... | collective-permute-start | bytes 2752520 | tf_op jit(solution)/shard_map/ppermute | solution.py:272
  785.0 104.5 %collective-permute-start.7 = (bf16[256,1792]{1,0:T(8,128)(2,1)S(1)}, bf16[256,1792]{1,0:T(8,128)(2,1)}, u32[]{:S(2)}, u32[]{:S(2)}) collective-permute-start(bf16[256,1792]{1,0:T(8,128)(2,1)S(1)} %get-tuple-element.67), channel_id=1, source_target_pairs={{0,2},{1,3},{2,0},{3,1},{4,6},{5,7},{6,4},{7,5},{8,10},{9,11},{10,... | collective-permute-start | bytes 2752520 | tf_op jit(solution)/shard_map/ppermute | solution.py:272
  (7 other events, 113.3 us)

commit v2 on v1

v2 whole, which is shorter than its diff:
```python
import functools

import jax
import jax.numpy as jnp
from jax import lax
from jax.experimental import pallas as pl
from jax.experimental.pallas import tpu as pltpu
from jax.sharding import PartitionSpec as P


HEAD_DIM = 128
TAU_CLIP = 100.0
ROPE_THETA = 50000.0
TILE_N = 256
CLIP_ROWS = 64
LOG2_E = 1.4426950408889634
VMEM_LIMIT = 62 * 1024 * 1024


def rope_tables(pos_ids):
    half_dim = HEAD_DIM // 2
    inv_freq = jnp.float32(ROPE_THETA) ** (-jnp.arange(half_dim, dtype=jnp.float32) * (2.0 / HEAD_DIM))
    angle = pos_ids.astype(jnp.float32)[:, None] * inv_freq[None, :]
    cos_t, sin_t = jnp.cos(angle), jnp.sin(angle)
    return jnp.concatenate([cos_t, cos_t], axis=-1), jnp.concatenate([-sin_t, sin_t], axis=-1)


def clip_rows(total, n_steps):
    return -(-total // (16 * n_steps)) * 16


class ClipPass:
    def __init__(self, step, n_steps, units, fac_ref, buf, in_sems, out_sems):
        self.step, self.n_steps, self.units = step, n_steps, units
        self.fac_ref, self.buf, self.in_sems, self.out_sems = fac_ref, buf, in_sems, out_sems
        self.rows, self.width = buf.shape[2], buf.shape[3]

    def strip(self, ref, col0, step):
        row0 = pl.multiple_of(jnp.minimum(step * self.rows, ref.shape[0] - self.rows), 16)
        return ref.at[pl.ds(row0, self.rows), pl.ds(col0, self.width)]

    def copies(self, step, inward):
        slot = lax.rem(step, 3)
        for u, (src, dst, col0, _) in enumerate(self.units):
            if inward:
                yield pltpu.make_async_copy(self.strip(src, col0, step), self.buf.at[slot, u], self.in_sems.at[slot, u])
            else:
                yield pltpu.make_async_copy(self.buf.at[slot, u], self.strip(dst, col0, step), self.out_sems.at[slot, u])

    def start(self, step, inward):
        for copy in self.copies(step, inward):
            copy.start()

    def wait(self, step, inward):
        for copy in self.copies(step, inward):
            copy.wait()

    def open(self):
        step = self.step

        @pl.when(step == 0)
        def _():
            self.start(step, True)

        @pl.when(step >= 2)
        def _():
            self.wait(step - 2, False)

        @pl.when(step + 1 < self.n_steps)
        def _():
            self.start(step + 1, True)

        self.wait(step, True)

    def scale(self, u):
        slot, row = lax.rem(self.step, 3), self.units[u][3]
        for c0 in range(0, self.width, HEAD_DIM):
            fac = self.fac_ref[row : row + 1, c0 : c0 + HEAD_DIM]
            for r0 in range(0, self.rows, CLIP_ROWS):
                at = (slot, u, slice(r0, min(r0 + CLIP_ROWS, self.rows)), slice(c0, c0 + HEAD_DIM))
                self.buf[at] = (self.buf[at].astype(jnp.float32) * fac).astype(self.buf.dtype)

    def close(self):
        step = self.step
        self.start(step, False)

        @pl.when(step == self.n_steps - 1)
        def _():
            self.wait(step - 1, False)
            self.wait(step, False)


def clip_scratch(n_units, rows, width):
    return [
        pltpu.VMEM((3, n_units, rows, width), jnp.bfloat16),
        pltpu.SemaphoreType.DMA((3, n_units)),
        pltpu.SemaphoreType.DMA((3, n_units)),
    ]


def proj_kernel(n_chunks, n_alias, tile0, clip_cols, idx_ref, *refs):
    pieces = refs[: 2 * n_chunks]
    n_in = 2 * n_chunks + 5 + (1 if clip_cols else 0)
    cos_ref, sin_ref, wq_hbm, wk_hbm, wv_hbm = refs[2 * n_chunks : 2 * n_chunks + 5]
    outs = refs[n_in + n_alias :]
    (q_ref, k_ref, v_ref), outs = outs[:3], outs[3:]
    if clip_cols:
        (wq_new, wk_new), outs = outs[:2], outs[2:]
    (x_scr, x_sems, w_scr, w_sems), outs = outs[:4], outs[4:]
    tile, chunk = pl.program_id(0), pl.program_id(1)
    n_tiles = pl.num_programs(0)
    rows = pieces[0].shape[0]
    core = idx_ref[0]
    half_cols = wq_hbm.shape[1] // 2

    def piece_copy(c, side):
        row0 = (core if side == 0 else 1 - core) * rows
        return pltpu.make_async_copy(
            pieces[2 * c + side], x_scr.at[c, pl.ds(pl.multiple_of(row0, rows), rows)], x_sems.at[c, side]
        )

    def weight_copy(w, at_tile):
        col0 = pl.multiple_of(core * half_cols + (tile0 + at_tile) * TILE_N, TILE_N)
        w_hbm = (wq_hbm, wk_hbm, wv_hbm)[w]
        return pltpu.make_async_copy(w_hbm.at[:, pl.ds(col0, TILE_N)], w_scr.at[w], w_sems.at[w])

    @pl.when(jnp.logical_and(tile == 0, chunk == 0))
    def _():
        for side in range(2):
            piece_copy(0, side).start()
        for w in range(3):
            weight_copy(w, 0).start()
        for c in range(1, n_chunks):
            for side in range(2):
                piece_copy(c, side).start()

    for c in range(n_chunks):

        @pl.when(jnp.logical_and(tile == 0, chunk == c))
        def _():
            for side in range(2):
                piece_copy(c, side).wait()

    clip = None
    if clip_cols:
        units = [(src, dst, col0, h) for src, dst in ((wq_hbm, wq_new), (wk_hbm, wk_new)) for h, col0 in enumerate(clip_cols)]
        clip = ClipPass(tile * n_chunks + chunk, n_tiles * n_chunks, units, refs[2 * n_chunks + 5], *outs)
        clip.open()

    for w, o_ref in enumerate((q_ref, k_ref, v_ref)):

        @pl.when(chunk == 0)
        def _():
            weight_copy(w, tile).wait()

        acc = jnp.dot(x_scr[chunk], w_scr[w], preferred_element_type=jnp.float32)
        if w < 2:
            cos_t, sin_t = cos_ref[0], sin_ref[0]
            for h in range(TILE_N // HEAD_DIM):
                cols = slice(h * HEAD_DIM, (h + 1) * HEAD_DIM)
                t = acc[:, cols]
                o_ref[0, :, cols] = (t * cos_t + pltpu.roll(t, HEAD_DIM // 2, 1) * sin_t).astype(o_ref.dtype)
        else:
            o_ref[0] = acc.astype(o_ref.dtype)
        if clip:
            for u in range(len(clip.units)):
                if min(u, 2) == w:
                    clip.scale(u)

        @pl.when(jnp.logical_and(chunk == n_chunks - 1, tile + 1 < n_tiles))
        def _():
            weight_copy(w, tile + 1).start()

    if clip:
        clip.close()


def project(idx, pieces, cos_t, sin_t, w_q, w_k, w_v, into, tile0, n_tiles, clip_cols=(), factor=None):
    n_chunks = len(pieces) // 2
    rows, depth = pieces[0].shape
    total_chunks = cos_t.shape[0]
    half_cols = w_q.shape[1] // 2
    table_spec = pl.BlockSpec((1, 2 * rows, HEAD_DIM), lambda n, c, idx: (idx[1 + c], 0, 0))
    o_spec = pl.BlockSpec((1, 2 * rows, TILE_N), lambda n, c, idx: (idx[1 + c], 0, tile0 + n))
    any_spec = pl.BlockSpec(memory_space=pl.ANY)
    n_alias = 0 if into is None else 3
    o_shape = jax.ShapeDtypeStruct((total_chunks, 2 * rows, half_cols), jnp.bfloat16)
    flops = 2 * 3 * n_chunks * 2 * rows * depth * n_tiles * TILE_N
    first_alias = 1 + 2 * n_chunks + 5 + (1 if clip_cols else 0)
    scratch = [
        pltpu.VMEM((n_chunks, 2 * rows, depth), jnp.bfloat16),
        pltpu.SemaphoreType.DMA((n_chunks, 2)),
        pltpu.VMEM((3, depth, TILE_N), jnp.bfloat16),
        pltpu.SemaphoreType.DMA((3,)),
    ]
    clip_specs, clip_args, clip_outs = [], [], []
    if clip_cols:
        clip_specs = [pl.BlockSpec(factor.shape, lambda n, c, idx: (0, 0))]
        clip_args = [factor]
        clip_outs = [jax.ShapeDtypeStruct(w_q.shape, w_q.dtype)] * 2
        scratch += clip_scratch(2 * len(clip_cols), clip_rows(depth, n_tiles * n_chunks), factor.shape[1])
    return pl.pallas_call(
        functools.partial(proj_kernel, n_chunks, n_alias, tile0, clip_cols),
        grid_spec=pltpu.PrefetchScalarGridSpec(
            num_scalar_prefetch=1,
            grid=(n_tiles, n_chunks),
            in_specs=[any_spec] * (2 * n_chunks) + [table_spec] * 2 + [any_spec] * 3 + clip_specs + [any_spec] * n_alias,
            out_specs=[o_spec] * 3 + [any_spec] * len(clip_outs),
            scratch_shapes=scratch,
        ),
        out_shape=[o_shape] * 3 + clip_outs,
        input_output_aliases={first_alias + i: i for i in range(n_alias)},
        compiler_params=pltpu.CompilerParams(
            dimension_semantics=("arbitrary", "arbitrary"), vmem_limit_bytes=VMEM_LIMIT
        ),
        cost_estimate=pl.CostEstimate(
            flops=flops, bytes_accessed=2 * 3 * depth * n_tiles * TILE_N + 2 * n_chunks * rows * depth * 2, transcendentals=0
        ),
    )(idx, *pieces, cos_t, sin_t, w_q, w_k, w_v, *clip_args, *(into or ()))


def attn_kernel(blk, q_ref, k_ref, v_ref, o_ref, m_ref, s_scr, p_scr):
    n_chunks, rows, _ = q_ref.shape
    per_chunk = rows // blk
    n_blocks = n_chunks * per_chunk
    scale = HEAD_DIM ** -0.5
    lanes = blk // HEAD_DIM if blk >= HEAD_DIM else 1
    width = blk // lanes
    causal = lax.broadcasted_iota(jnp.int32, (blk, blk), 0) >= lax.broadcasted_iota(jnp.int32, (blk, blk), 1)

    def rows_of(ref, i):
        r0 = (i % per_chunk) * blk
        return ref[i // per_chunk, r0 : r0 + blk, :]

    def scores(i):
        q = rows_of(q_ref, i)
        lane_max = None
        for j in range(i + 1):
            s = lax.dot_general(q, rows_of(k_ref, j), (((1,), (1,)), ((), ())), preferred_element_type=jnp.float32)
            if j == i:
                s = jnp.where(causal, s, -jnp.inf)
            s_scr[i % 2, :, j * blk : (j + 1) * blk] = s
            for c in range(lanes):
                part = s[:, c * width : (c + 1) * width]
                lane_max = part if lane_max is None else jnp.maximum(lane_max, part)
        return jnp.max(lane_max, axis=-1, keepdims=True)

    row_max = scores(0)
    head_max = row_max
    for i in range(n_blocks):
        if i + 1 < n_blocks:
            next_max = scores(i + 1)
            head_max = jnp.maximum(head_max, next_max)
        lane_sum = None
        for j in range(i + 1):
            cols = slice(j * blk, (j + 1) * blk)
            p = jnp.exp2((s_scr[i % 2, :, cols] - row_max) * (scale * LOG2_E))
            for c in range(lanes):
                part = p[:, c * width : (c + 1) * width]
                lane_sum = part if lane_sum is None else lane_sum + part
            p_scr[i % 2, :, cols] = p.astype(p_scr.dtype)
        keys = (i + 1) * blk
        values = v_ref[...].reshape(n_chunks * rows, HEAD_DIM)[:keys]
        acc = jnp.dot(p_scr[i % 2, :, :keys], values, preferred_element_type=jnp.float32)
        row_sum = jnp.sum(lane_sum, axis=-1, keepdims=True)
        r0 = (i % per_chunk) * blk
        o_ref[i // per_chunk, r0 : r0 + blk, :] = (acc / row_sum).astype(o_ref.dtype)
        if i + 1 < n_blocks:
            row_max = next_max
    m_ref[...] = jnp.broadcast_to(jnp.max(head_max, axis=0, keepdims=True) * scale, m_ref.shape)


def attend(q, k, v, head0, n_heads):
    n_chunks, rows, _ = q.shape
    blk = min(256, rows)
    in_spec = pl.BlockSpec((n_chunks, rows, HEAD_DIM), lambda h: (0, 0, head0 + h))
    o_spec = pl.BlockSpec((n_chunks, rows, HEAD_DIM), lambda h: (0, 0, h))
    seq = n_chunks * rows
    return pl.pallas_call(
        functools.partial(attn_kernel, blk),
        grid=(n_heads,),
        in_specs=[in_spec] * 3,
        out_specs=[o_spec, pl.BlockSpec((8, HEAD_DIM), lambda h: (h, 0))],
        out_shape=[
            jax.ShapeDtypeStruct((n_chunks, rows, n_heads * HEAD_DIM), jnp.bfloat16),
            jax.ShapeDtypeStruct((8 * n_heads, HEAD_DIM), jnp.float32),
        ],
        scratch_shapes=[pltpu.VMEM((2, blk, seq), jnp.float32), pltpu.VMEM((2, blk, seq), jnp.bfloat16)],
        compiler_params=pltpu.CompilerParams(dimension_semantics=("arbitrary",), vmem_limit_bytes=VMEM_LIMIT),
        cost_estimate=pl.CostEstimate(
            flops=8 * seq * seq * HEAD_DIM * n_heads // 2,
            bytes_accessed=8 * seq * HEAD_DIM * n_heads,
            transcendentals=seq * seq * n_heads // 2,
        ),
    )(q, k, v)


def out_kernel(n_chunks, col_offs, n_alias, clip_cols, idx_ref, *refs):
    n_groups = len(col_offs)
    n_pieces = n_chunks * 2 * n_groups
    pieces = refs[:n_pieces]
    wo_ref, fac_ref, wc_hbm = refs[n_pieces : n_pieces + 3]
    o_hbm, c_hbm, a_scr, o_scr, a_sems, o_sems, *clip_refs = refs[n_pieces + 3 + n_alias :]
    tile, n_tiles = pl.program_id(0), pl.num_programs(0)
    core = idx_ref[0]
    rows = pieces[0].shape[0]
    half_cols = a_scr.shape[1] // 2

    def piece_copies():
        copies = []
        for c in range(n_chunks):
            for side in range(2):
                for g in range(n_groups):
                    n = (c * 2 + side) * n_groups + g
                    col0 = (core if side == 0 else 1 - core) * half_cols + col_offs[g]
                    width = pieces[n].shape[1]
                    copies.append(
                        pltpu.make_async_copy(
                            pieces[n],
                            a_scr.at[pl.ds(c * rows, rows), pl.ds(pl.multiple_of(col0, HEAD_DIM), width)],
                            a_sems.at[n],
                        )
                    )
        return copies

    def out_copies(slot, at_tile):
        return [
            pltpu.make_async_copy(
                o_scr.at[slot, pl.ds(c * rows, rows)],
                o_hbm.at[idx_ref[1 + c], :, pl.ds(pl.multiple_of(at_tile * TILE_N, TILE_N), TILE_N)],
                o_sems.at[slot, c],
            )
            for c in range(n_chunks)
        ]

    @pl.when(tile == 0)
    def _():
        for copy in piece_copies():
            copy.start()

    clip = ClipPass(tile, n_tiles, [(wc_hbm, c_hbm, col0, h) for h, col0 in enumerate(clip_cols)], fac_ref, *clip_refs)
    clip.open()

    @pl.when(tile == 0)
    def _():
        for copy in piece_copies():
            copy.wait()

    slot = lax.rem(tile, 2)

    @pl.when(tile >= 2)
    def _():
        for copy in out_copies(slot, tile - 2):
            copy.wait()

    o_scr[slot] = jnp.dot(a_scr[...], wo_ref[...], preferred_element_type=jnp.float32).astype(o_scr.dtype)
    for u in range(len(clip.units)):
        clip.scale(u)
    for copy in out_copies(slot, tile):
        copy.start()
    clip.close()

    @pl.when(tile == n_tiles - 1)
    def _():
        for copy in out_copies(1 - slot, tile - 1):
            copy.wait()
        for copy in out_copies(slot, tile):
            copy.wait()


def out_project(idx, pieces, col_offs, w_o, factor, w_clip, clip_into, clip_cols, into, out_shape):
    n_groups = len(col_offs)
    n_chunks = len(pieces) // (2 * n_groups)
    rows = pieces[0].shape[0]
    depth, width = w_o.shape
    n_tiles = width // TILE_N
    any_spec = pl.BlockSpec(memory_space=pl.ANY)
    tile_spec = pl.BlockSpec((depth, TILE_N), lambda n, idx: (0, n))
    alias_at = 1 + len(pieces) + 3
    aliased, aliases = [clip_into], {alias_at: 1}
    if into is not None:
        aliased, aliases = [clip_into, into], {alias_at: 1, alias_at + 1: 0}
    return pl.pallas_call(
        functools.partial(out_kernel, n_chunks, col_offs, len(aliased), clip_cols),
        grid_spec=pltpu.PrefetchScalarGridSpec(
            num_scalar_prefetch=1,
            grid=(n_tiles,),
            in_specs=[any_spec] * len(pieces)
            + [tile_spec, pl.BlockSpec(factor.shape, lambda n, idx: (0, 0)), any_spec]
            + [any_spec] * len(aliased),
            out_specs=[any_spec, any_spec],
            scratch_shapes=[
                pltpu.VMEM((n_chunks * rows, depth), jnp.bfloat16),
                pltpu.VMEM((2, n_chunks * rows, TILE_N), jnp.bfloat16),
                pltpu.SemaphoreType.DMA((len(pieces),)),
                pltpu.SemaphoreType.DMA((2, n_chunks)),
            ]
            + clip_scratch(len(clip_cols), clip_rows(w_clip.shape[0], n_tiles), factor.shape[1]),
        ),
        out_shape=[jax.ShapeDtypeStruct(out_shape, jnp.bfloat16), jax.ShapeDtypeStruct(w_clip.shape, jnp.bfloat16)],
        input_output_aliases=aliases,
        compiler_params=pltpu.CompilerParams(dimension_semantics=("arbitrary",), vmem_limit_bytes=VMEM_LIMIT),
        cost_estimate=pl.CostEstimate(
            flops=2 * n_chunks * rows * depth * width, bytes_accessed=2 * 2 * depth * width, transcendentals=0
        ),
    )(idx, *pieces, w_o, factor, w_clip, *aliased)


def solution(mesh):
    cp_size = mesh.shape["cp"]
    n_chips = cp_size // 2

    def permute(x, flip):
        return lax.ppermute(x, "cp", [(src, src ^ flip) for src in range(cp_size)])

    def device_body(hidden, pos_ids, w_q, w_k, w_v, w_o):
        cp_rank = lax.axis_index("cp")
        core, chip = cp_rank % 2, cp_rank // 2
        n_heads = w_q.shape[1] // HEAD_DIM
        half_heads = n_heads // 2
        half_tiles = half_heads * HEAD_DIM // TILE_N
        tiles_a = (half_tiles + 1) // 2
        heads_per_tile = TILE_N // HEAD_DIM
        groups = [(0, tiles_a), (tiles_a, half_tiles - tiles_a)]
        col_offs = tuple(t0 * TILE_N for t0, _ in groups)

        def index(*offsets):
            return jnp.stack([core] + [chip ^ d for d in offsets]).astype(jnp.int32)

        all_pos = lax.all_gather(pos_ids, "cp", tiled=True)
        cos_t, sin_t = (t.reshape(n_chips, -1, HEAD_DIM) for t in rope_tables(all_pos))

        same, other = {}, {}
        for d in range(n_chips):
            row = lax.dynamic_index_in_dim(hidden, chip ^ d, 0, keepdims=False)
            same[d] = permute(row, 2 * d) if d else row
            other[d] = permute(same[d], 1)

        def fill(qkv, offsets, tile0, n_tiles, *clip):
            pieces = [piece for d in offsets for piece in (same[d], other[d])]
            return project(index(*offsets), pieces, cos_t, sin_t, w_q, w_k, w_v, qkv, tile0, n_tiles, *clip)

        rest = tuple(range(1, n_chips))
        split = half_tiles - max(half_tiles // 4, 1)
        qkv = fill(None, (0,), 0, split)
        qkv = fill(qkv, (0,), split, half_tiles - split)
        qkv = fill(qkv, rest[:-1], *groups[0])
        qkv = fill(qkv, rest[-1:], *groups[0])

        sent, maxes, factors, clip_cols = [], [], [], []
        for g, (tile0, n_tiles) in enumerate(groups):
            n_group = n_tiles * heads_per_tile
            if g == 1:
                *qkv, w_q_new, w_k_new = fill(qkv, rest, tile0, n_tiles, clip_cols[0], factors[0])
            vals, row_max = attend(*qkv, tile0 * heads_per_tile, n_group)
            local_max = jnp.max(row_max.reshape(n_group, -1), axis=1)
            spread = jnp.where(jnp.arange(2)[:, None] == core, local_max[None, :], -jnp.inf)
            group_max = lax.pmax(spread, ("dp", "cp"))
            maxes.append(group_max)
            factor = jnp.where(group_max > TAU_CLIP, jnp.sqrt(TAU_CLIP / group_max), 1.0)
            factors.append(jnp.repeat(factor, HEAD_DIM, axis=1))
            clip_cols.append(tuple((h * half_tiles + tile0) * TILE_N for h in range(2)))
            vals = vals.reshape(cp_size, -1, vals.shape[-1])
            got = {}
            for d in range(n_chips):
                for side in range(2):
                    piece = lax.dynamic_index_in_dim(vals, cp_rank ^ (2 * d + side), 0, keepdims=False)
                    got[d, side] = permute(piece, 2 * d + side) if d or side else piece
            sent.append(got)
        head_max = jnp.concatenate(maxes, axis=1).reshape(n_heads)

        def out_rows(offsets, w_clip, clip_into, into):
            pieces = [sent[g][d, side] for d in offsets for side in range(2) for g in range(len(groups))]
            return out_project(
                index(*offsets), pieces, col_offs, w_o, factors[1], w_clip, clip_into, clip_cols[1], into, hidden.shape
            )

        attn_out, w_q_new = out_rows((0,), w_q, w_q_new, None)
        attn_out, w_k_new = out_rows(rest, w_k, w_k_new, attn_out)
        return attn_out, head_max, w_q_new, w_k_new

    return jax.shard_map(
        device_body,
        mesh=mesh,
        in_specs=(P("dp", "cp", None), P("cp"), P(None, None), P(None, None), P(None, None), P(None, None)),
        out_specs=(P("dp", "cp", None), P(None), P(None, None), P(None, None)),
        check_vma=False,
    )
```

time: 1010 us -> 1150 us (1.14)
  Pallas kernels: 697 us -> 804 us
  blocking collectives: 195 us -> 228 us
    pallas_call x8 -> x7, Pallas kernels: 574 us -> 712 us  [the longest x5 552 us: project(): pl.pallas_call(functools.partial(proj_kernel, n_chunks, n_alias, tile0, c...]
    pmax x1 -> x2, blocking collectives: 44.3 us -> 75.8 us  [device_body(): group_max = lax.pmax(spread, ('dp', 'cp'))]
    pallas_call x2, Pallas kernels: 123 us -> 92.7 us  [attend(): pl.pallas_call(functools.partial(attn_kernel, blk), grid=(n_heads,), in_s...]
  transfers between devices with their start and end apart: 21 -> 21, of which waited for: 3 -> 3; matrix products, arithmetic and copies ran while one was open for 2% -> 1% of each run, Pallas kernels for 30% -> 30%
where the time goes in v2:
time: 1150 us
  Pallas kernels  804 us (70%)
  blocking collectives  228 us (20%)
  waiting for transfers between devices  58.1 us (5%)
  local copies, waits for them, and re-layouts  23 us (2%)
  starting transfers between devices  22.9 us (2%)
    pallas_call x5, Pallas kernels, project(): pl.pallas_call(functools.partial(proj_kernel, n_chunks, n_alias, tile0, c...  552 us
    pallas_call x2, Pallas kernels, out_project(): pl.pallas_call(functools.partial(out_kernel, n_chunks, col_offs, len(alia...  159 us
    all_gather x1, blocking collectives, device_body(): all_pos = lax.all_gather(pos_ids, 'cp', tiled=True)  152 us
    pallas_call x2, Pallas kernels, attend(): pl.pallas_call(functools.partial(attn_kernel, blk), grid=(n_heads,), in_s...  92.7 us
    pmax x2, blocking collectives, device_body(): group_max = lax.pmax(spread, ('dp', 'cp'))  75.8 us
    ppermute x21, waiting for transfers between devices, permute(): return lax.ppermute(x, 'cp', [(src, src ^ flip) for src in range(cp_size)])  58.1 us
  transfers between devices with their start and end apart: 21, of which 3 were waited for; matrix products, arithmetic and copies ran while one was open for 1% of the time, Pallas kernels for 30%

profile of v2, /device:TPU:0, one launch (start us, length us, event | category | flops | bytes accessed | tf_op | source)
XLA Modules:
  0.0 1147.1 jit_solution(16160811765007724779)
XLA Ops:
  0.7 9.2 dynamic-slice_bitcast_fusion
  9.9 3.2 collective-permute-start.2
  14.6 152.1 %all-gather = s32[8,1,256]{2,1,0:T(1,128)S(1)} all-gather(s32[1,1,256]{2,1,0:T(1,128)S(1)} %bitcast.63), channel_id=1, replica_groups=mesh['dp'=2,'cp'=8] {'cp'}, dimensions={0}, use_global_device_ids=true | all-gather | bytes 9216 | tf_op jit(solution)/shard_map/all_gather | solution.py:430
  169.3 3.7 fusion
  175.9 103.3 %shard_map.93 = (bf16[4,512,3328]{2,1,0:T(8,128)(2,1)}, bf16[4,512,3328]{2,1,0:T(8,128)(2,1)}, bf16[4,512,3328]{2,1,0:T(8,128)(2,1)}) custom-call(s32[2]{0:T(128)} %get-tuple-element.78.idx_ref, bf16[256,6656]{1,0:T(8,128)(2,1)} %copy-done, bf16[256,6656]{1,0:T(8,128)(2,1)} %collective-permute-done.6.refs_1_, ...), custom_call_target="tpu_custom_call" | custom-call | flops 52344913920 | bytes 109051904 | tf_op jit(solution)/shard_map/pallas_call | solution.py:202
  279.2 36.7 %shard_map.94 = (bf16[4,512,3328]{2,1,0:T(8,128)(2,1)}, bf16[4,512,3328]{2,1,0:T(8,128)(2,1)}, bf16[4,512,3328]{2,1,0:T(8,128)(2,1)}) custom-call(s32[2]{0:T(128)} %get-tuple-element.78.idx_ref, bf16[256,6656]{1,0:T(8,128)(2,1)} %copy-done, ...), custom_call_target="tpu_custom_call", output_to_operand_aliasing={{0}: (8, {}), {1}: (9, {}), {2}: (10, {})} | custom-call | flops 15703474176 | bytes 37486592 | tf_op jit(solution)/shard_map/pallas_call | solution.py:202
  315.9 139.2 %shard_map.95 = (bf16[4,512,3328]{2,1,0:T(8,128)(2,1)}, bf16[4,512,3328]{2,1,0:T(8,128)(2,1)}, bf16[4,512,3328]{2,1,0:T(8,128)(2,1)}) custom-call(s32[3]{0:T(128)} %pad_add_fusion.2.idx_ref, bf16[256,6656]{1,0:T(8,128)(2,1)} %collective-permute-done.2.refs_0_, ...), custom_call_target="tpu_custom_call", output_to_operand_aliasing={{0}: (10, {}), {1}: (11, {}), {2}: (12, {})} | custom-call | flops 73282879488 | bytes 85196800 | tf_op jit(solution)/shard_map/pallas_call | solution.py:202
  455.1 74.6 %shard_map.96 = (bf16[4,512,3328]{2,1,0:T(8,128)(2,1)}, bf16[4,512,3328]{2,1,0:T(8,128)(2,1)}, bf16[4,512,3328]{2,1,0:T(8,128)(2,1)}) custom-call(s32[2]{0:T(128)} %get-tuple-element.77.idx_ref, bf16[256,6656]{1,0:T(8,128)(2,1)} %collective-permute-done.refs_0_.refs_4_, ...), custom_call_target="tpu_custom_call", output_to_operand_aliasing={{0}: (8, {}), {1}: (9, {}), {2}: (10, {})} | custom-call | flops 36641439744 | bytes 78381056 | tf_op jit(solution)/shard_map/pallas_call | solution.py:202
  529.8 49.7 %shard_map.97 = (bf16[4,512,1792]{2,1,0:T(8,128)(2,1)}, f32[112,128]{1,0:T(8,128)}) custom-call(bf16[4,512,3328]{2,1,0:T(8,128)(2,1)} %get-tuple-element.38.q_ref.refs_12_, bf16[4,512,3328]{2,1,0:T(8,128)(2,1)} %get-tuple-element.39.k_ref.refs_13_, bf16[4,512,3328]{2,1,0:T(8,128)(2,1)} %get-tuple-element.40.v_ref.refs_14_), custom_call_target="tpu_custom_call" | custom-call | flops 30064771072 | bytes 29360128 | tf_op jit(solution)/shard_map/pallas_call | solution.py:279
  580.8 32.1 %pmax.14 = f32[2,14]{1,0:T(2,128)S(1)} all-reduce(f32[2,14]{1,0:T(2,128)S(1)} %broadcast_select_fusion.1), channel_id=1, replica_groups=mesh['dp'=2,'cp'=8] {'dp','cp'}, use_global_device_ids=true, to_apply=%region_2.3 | all-reduce | flops 28 | bytes 224 | tf_op jit(solution)/shard_map/pmax | solution.py:458
  613.6 198.4 %shard_map.98 = (bf16[4,512,3328]{2,1,0:T(8,128)(2,1)}, bf16[4,512,3328]{2,1,0:T(8,128)(2,1)}, bf16[4,512,3328]{2,1,0:T(8,128)(2,1)}, bf16[6656,6656]{1,0:T(8,128)(2,1)}, bf16[6656,6656]{1,0:T(8,128)(2,1)}) custom-call(s32[4]{0:T(128)} %pad_add_fusion.idx_ref, ...), custom_call_target="tpu_custom_call", output_to_operand_aliasing={{0}: (13, {}), {1}: (14, {}), {2}: (15, {})} | custom-call | flops 94220845056 | bytes 81788928 | tf_op jit(solution)/shard_map/pallas_call | solution.py:202
  812.0 43.0 %shard_map.99 = (bf16[4,512,1536]{2,1,0:T(8,128)(2,1)}, f32[96,128]{1,0:T(8,128)}) custom-call(bf16[4,512,3328]{2,1,0:T(8,128)(2,1)} %get-tuple-element.43.q_ref, bf16[4,512,3328]{2,1,0:T(8,128)(2,1)} %get-tuple-element.44.k_ref, bf16[4,512,3328]{2,1,0:T(8,128)(2,1)} %get-tuple-element.45.v_ref), custom_call_target="tpu_custom_call" | custom-call | flops 25769803776 | bytes 25165824 | tf_op jit(solution)/shard_map/pallas_call | solution.py:279
  855.0 4.9 dynamic-slice_bitcast_fusion.12
  859.8 2.3 collective-permute-start.18
  864.5 5.9 dynamic-slice_bitcast_fusion.4
  873.1 7.0 collective-permute-done.18.refs_11_
  880.1 2.2 collective-permute-start.12
  882.3 16.0 %collective-permute-done.16.refs_9_ = bf16[256,1536]{1,0:T(8,128)(2,1)} collective-permute-done((bf16[256,1536]{1,0:T(8,128)(2,1)S(1)}, bf16[256,1536]{1,0:T(8,128)(2,1)}, u32[]{:S(2)}, u32[]{:S(2)}) %collective-permute-start.16) | collective-permute-done | bytes 786464 | tf_op jit(solution)/shard_map/ppermute | solution.py:414
  898.9 35.1 %collective-permute-done.14.refs_7_ = bf16[256,1536]{1,0:T(8,128)(2,1)} collective-permute-done((bf16[256,1536]{1,0:T(8,128)(2,1)S(1)}, bf16[256,1536]{1,0:T(8,128)(2,1)}, u32[]{:S(2)}, u32[]{:S(2)}) %collective-permute-start.14) | collective-permute-done | bytes 786464 | tf_op jit(solution)/shard_map/ppermute | solution.py:414
  934.0 2.3 collective-permute-start.8
  936.7 43.7 %pmax.15 = f32[2,12]{1,0:T(2,128)S(1)} all-reduce(f32[2,12]{1,0:T(2,128)S(1)} %broadcast_select_fusion), channel_id=1, replica_groups=mesh['dp'=2,'cp'=8] {'dp','cp'}, use_global_device_ids=true, to_apply=%region_5.6 | all-reduce | flops 24 | bytes 192 | tf_op jit(solution)/shard_map/pmax | solution.py:458
  981.7 2.2 collective-permute-start.15
  987.5 68.7 %shard_map.100 = (bf16[4,256,6656]{2,1,0:T(8,128)(2,1)}, bf16[6656,6656]{1,0:T(8,128)(2,1)}) custom-call(s32[2]{0:T(128)} %get-tuple-element.78.idx_ref, bf16[256,1792]{1,0:T(8,128)(2,1)} %get-tuple-element.59.refs_0_, bf16[256,1536]{1,0:T(8,128)(2,1)} %get-tuple-element.67.refs_1_, bf16[256,1792]{1,0:T(8,128)(2,1)} %copy-done.2, ...), custom_call_target="tpu_custom_call", output_to_operand_aliasing={{1}: (8, {})} | custom-call | flops 22682796032 | bytes 177209344 | tf_op jit(solution)/shard_map/pallas_call | solution.py:383
  1056.3 90.5 %shard_map.101 = (bf16[4,256,6656]{2,1,0:T(8,128)(2,1)}, bf16[6656,6656]{1,0:T(8,128)(2,1)}) custom-call(s32[4]{0:T(128)} %pad_add_fusion.idx_ref, bf16[256,1792]{1,0:T(8,128)(2,1)} %collective-permute-done.7.refs_0_, bf16[256,1536]{1,0:T(8,128)(2,1)} %collective-permute-done.8.refs_1_, ...), custom_call_target="tpu_custom_call", output_to_operand_aliasing={{1}: (16, {}), {0}: (17, {})} | custom-call | flops 68048388096 | bytes 177209344 | tf_op jit(solution)/shard_map/pallas_call | solution.py:383
  (72 shorter events, 19.6 us)
Async XLA Ops:
  9.9 165.1 %collective-permute-start.2 = (bf16[256,6656]{1,0:T(8,128)(2,1)}, bf16[256,6656]{1,0:T(8,128)(2,1)}, u32[]{:S(2)}, u32[]{:S(2)}) collective-permute-start(bf16[256,6656]{1,0:T(8,128)(2,1)} %get-tuple-element.55), channel_id=1, source_target_pairs={{0,2},{1,3},{2,0},{3,1},{4,6},{5,7},{6,4},{7,5},{8,10},{9,11},{10,... | collective-permute-start | bytes 10223624 | tf_op jit(solution)/shard_map/ppermute | solution.py:414
  13.1 162.2 %collective-permute-start = (bf16[256,6656]{1,0:T(8,128)(2,1)}, bf16[256,6656]{1,0:T(8,128)(2,1)}, u32[]{:S(2)}, u32[]{:S(2)}) collective-permute-start(bf16[256,6656]{1,0:T(8,128)(2,1)} %get-tuple-element.56), channel_id=1, source_target_pairs={{0,6},{1,7},{2,4},{3,5},{4,2},{5,3},{6,0},{7,1},{8,14},{9,15},{10,... | collective-permute-start | bytes 10223624 | tf_op jit(solution)/shard_map/ppermute | solution.py:414
  14.6 160.9 %collective-permute-start.4 = (bf16[256,6656]{1,0:T(8,128)(2,1)}, bf16[256,6656]{1,0:T(8,128)(2,1)}, u32[]{:S(2)}, u32[]{:S(2)}) collective-permute-start(bf16[256,6656]{1,0:T(8,128)(2,1)} %get-tuple-element.57), channel_id=1, source_target_pairs={{0,4},{1,5},{2,6},{3,7},{4,0},{5,1},{6,2},{7,3},{8,12},{9,13},{10,... | collective-permute-start | bytes 10223624 | tf_op jit(solution)/shard_map/ppermute | solution.py:414
  14.6 161.2 %collective-permute-start.6 = (bf16[256,6656]{1,0:T(8,128)(2,1)S(1)}, bf16[256,6656]{1,0:T(8,128)(2,1)}, u32[]{:S(2)}, u32[]{:S(2)}) collective-permute-start(bf16[256,6656]{1,0:T(8,128)(2,1)S(1)} %get-tuple-element.54.refs_0_), channel_id=1, source_target_pairs={{0,1},{1,0},{2,3},{3,2},{4,5},{5,4},{6,7},{7,6},{8,9},{9,8},{10,11... | collective-permute-start | bytes 10223624 | tf_op jit(solution)/shard_map/ppermute | solution.py:414
  175.0 140.9 %collective-permute-start.3 = (bf16[256,6656]{1,0:T(8,128)(2,1)}, bf16[256,6656]{1,0:T(8,128)(2,1)}, u32[]{:S(2)}, u32[]{:S(2)}) collective-permute-start(bf16[256,6656]{1,0:T(8,128)(2,1)} %collective-permute-done.2.refs_0_), channel_id=1, source_target_pairs={{0,1},{1,0},{2,3},{3,2},{4,5},{5,4},{6,7},{7,6},{8,9},{9,8},{10,11... | collective-permute-start | bytes 10223624 | tf_op jit(solution)/shard_map/ppermute | solution.py:414
  175.3 279.8 %collective-permute-start.1 = (bf16[256,6656]{1,0:T(8,128)(2,1)}, bf16[256,6656]{1,0:T(8,128)(2,1)}, u32[]{:S(2)}, u32[]{:S(2)}) collective-permute-start(bf16[256,6656]{1,0:T(8,128)(2,1)} %collective-permute-done.refs_0_.refs_4_), channel_id=1, source_target_pairs={{0,1},{1,0},{2,3},{3,2},{4,5},{5,4},{6,7},{7,6},{8,9},{9,8},{10,11... | collective-permute-start | bytes 10223624 | tf_op jit(solution)/shard_map/ppermute | solution.py:414
  175.5 140.4 %collective-permute-start.5 = (bf16[256,6656]{1,0:T(8,128)(2,1)}, bf16[256,6656]{1,0:T(8,128)(2,1)}, u32[]{:S(2)}, u32[]{:S(2)}) collective-permute-start(bf16[256,6656]{1,0:T(8,128)(2,1)} %collective-permute-done.4.refs_2_), channel_id=1, source_target_pairs={{0,1},{1,0},{2,3},{3,2},{4,5},{5,4},{6,7},{7,6},{8,9},{9,8},{10,11... | collective-permute-start | bytes 10223624 | tf_op jit(solution)/shard_map/ppermute | solution.py:414
  529.8 50.9 %copy-start.5 = (pred[2]{0:T(512)(128)(4,1)S(1)}, pred[2]{0:T(512)(128)(4,1)}, u32[]{:S(2)}) copy-start(pred[2]{0:T(512)(128)(4,1)} %iota_compare_fusion) | copy-start | bytes 10
  855.0 81.3 %copy-start.4 = (f32[96,128]{1,0:T(8,128)S(1)}, f32[96,128]{1,0:T(8,128)}, u32[]{:S(2)}) copy-start(f32[96,128]{1,0:T(8,128)} %get-tuple-element.47) | copy-start | bytes 147460
  859.8 11.3 collective-permute-start.20
  859.8 20.3 %collective-permute-start.18 = (bf16[256,1536]{1,0:T(8,128)(2,1)S(1)}, bf16[256,1536]{1,0:T(8,128)(2,1)}, u32[]{:S(2)}, u32[]{:S(2)}) collective-permute-start(bf16[256,1536]{1,0:T(8,128)(2,1)S(1)} %get-tuple-element.68), channel_id=1, source_target_pairs={{0,7},{1,6},{2,5},{3,4},{4,3},{5,2},{6,1},{7,0},{8,15},{9,14},{10,... | collective-permute-start | bytes 2359304 | tf_op jit(solution)/shard_map/ppermute | solution.py:414
  862.2 36.1 %collective-permute-start.16 = (bf16[256,1536]{1,0:T(8,128)(2,1)S(1)}, bf16[256,1536]{1,0:T(8,128)(2,1)}, u32[]{:S(2)}, u32[]{:S(2)}) collective-permute-start(bf16[256,1536]{1,0:T(8,128)(2,1)S(1)} %get-tuple-element.69), channel_id=1, source_target_pairs={{0,6},{1,7},{2,4},{3,5},{4,2},{5,3},{6,0},{7,1},{8,14},{9,15},{10,... | collective-permute-start | bytes 2359304 | tf_op jit(solution)/shard_map/ppermute | solution.py:414
  862.9 71.1 %collective-permute-start.14 = (bf16[256,1536]{1,0:T(8,128)(2,1)S(1)}, bf16[256,1536]{1,0:T(8,128)(2,1)}, u32[]{:S(2)}, u32[]{:S(2)}) collective-permute-start(bf16[256,1536]{1,0:T(8,128)(2,1)S(1)} %get-tuple-element.70), channel_id=1, source_target_pairs={{0,5},{1,4},{2,7},{3,6},{4,1},{5,0},{6,3},{7,2},{8,13},{9,12},{10,... | collective-permute-start | bytes 2359304 | tf_op jit(solution)/shard_map/ppermute | solution.py:414
  870.3 115.2 %collective-permute-start.19 = (bf16[256,1792]{1,0:T(8,128)(2,1)}, bf16[256,1792]{1,0:T(8,128)(2,1)S(1)}, u32[]{:S(2)}, u32[]{:S(2)}) collective-permute-start(bf16[256,1792]{1,0:T(8,128)(2,1)} %get-tuple-element.58), channel_id=1, source_target_pairs={{0,1},{1,0},{2,3},{3,2},{4,5},{5,4},{6,7},{7,6},{8,9},{9,8},{10,11... | collective-permute-start | bytes 2752520 | tf_op jit(solution)/shard_map/ppermute | solution.py:414
  872.1 114.9 %collective-permute-start.17 = (bf16[256,1792]{1,0:T(8,128)(2,1)S(1)}, bf16[256,1792]{1,0:T(8,128)(2,1)S(1)}, u32[]{:S(2)}, u32[]{:S(2)}) collective-permute-start(bf16[256,1792]{1,0:T(8,128)(2,1)S(1)} %get-tuple-element.60), channel_id=1, source_target_pairs={{0,7},{1,6},{2,5},{3,4},{4,3},{5,2},{6,1},{7,0},{8,15},{9,14},{10,... | collective-permute-start | bytes 2752520 | tf_op jit(solution)/shard_map/ppermute | solution.py:414
  880.1 101.6 %collective-permute-start.12 = (bf16[256,1536]{1,0:T(8,128)(2,1)}, bf16[256,1536]{1,0:T(8,128)(2,1)}, u32[]{:S(2)}, u32[]{:S(2)}) collective-permute-start(bf16[256,1536]{1,0:T(8,128)(2,1)} %get-tuple-element.71), channel_id=1, source_target_pairs={{0,4},{1,5},{2,6},{3,7},{4,0},{5,1},{6,2},{7,3},{8,12},{9,13},{10,... | collective-permute-start | bytes 2359304 | tf_op jit(solution)/shard_map/ppermute | solution.py:414
  898.3 85.6 %collective-permute-start.10 = (bf16[256,1536]{1,0:T(8,128)(2,1)}, bf16[256,1536]{1,0:T(8,128)(2,1)}, u32[]{:S(2)}, u32[]{:S(2)}) collective-permute-start(bf16[256,1536]{1,0:T(8,128)(2,1)} %get-tuple-element.72), channel_id=1, source_target_pairs={{0,3},{1,2},{2,1},{3,0},{4,7},{5,6},{6,5},{7,4},{8,11},{9,10},{10,... | collective-permute-start | bytes 2359304 | tf_op jit(solution)/shard_map/ppermute | solution.py:414
  934.0 50.0 %collective-permute-start.8 = (bf16[256,1536]{1,0:T(8,128)(2,1)}, bf16[256,1536]{1,0:T(8,128)(2,1)}, u32[]{:S(2)}, u32[]{:S(2)}) collective-permute-start(bf16[256,1536]{1,0:T(8,128)(2,1)} %get-tuple-element.73), channel_id=1, source_target_pairs={{0,2},{1,3},{2,0},{3,1},{4,6},{5,7},{6,4},{7,5},{8,10},{9,11},{10,... | collective-permute-start | bytes 2359304 | tf_op jit(solution)/shard_map/ppermute | solution.py:414
  981.7 74.5 %collective-permute-start.15 = (bf16[256,1792]{1,0:T(8,128)(2,1)}, bf16[256,1792]{1,0:T(8,128)(2,1)}, u32[]{:S(2)}, u32[]{:S(2)}) collective-permute-start(bf16[256,1792]{1,0:T(8,128)(2,1)} %get-tuple-element.61), channel_id=1, source_target_pairs={{0,6},{1,7},{2,4},{3,5},{4,2},{5,3},{6,0},{7,1},{8,14},{9,15},{10,... | collective-permute-start | bytes 2752520 | tf_op jit(solution)/shard_map/ppermute | solution.py:414
  984.0 72.3 %collective-permute-start.13 = (bf16[256,1792]{1,0:T(8,128)(2,1)}, bf16[256,1792]{1,0:T(8,128)(2,1)}, u32[]{:S(2)}, u32[]{:S(2)}) collective-permute-start(bf16[256,1792]{1,0:T(8,128)(2,1)} %get-tuple-element.62), channel_id=1, source_target_pairs={{0,5},{1,4},{2,7},{3,6},{4,1},{5,0},{6,3},{7,2},{8,13},{9,12},{10,... | collective-permute-start | bytes 2752520 | tf_op jit(solution)/shard_map/ppermute | solution.py:414
  984.0 72.3 %collective-permute-start.11 = (bf16[256,1792]{1,0:T(8,128)(2,1)}, bf16[256,1792]{1,0:T(8,128)(2,1)}, u32[]{:S(2)}, u32[]{:S(2)}) collective-permute-start(bf16[256,1792]{1,0:T(8,128)(2,1)} %get-tuple-element.63), channel_id=1, source_target_pairs={{0,4},{1,5},{2,6},{3,7},{4,0},{5,1},{6,2},{7,3},{8,12},{9,13},{10,... | collective-permute-start | bytes 2752520 | tf_op jit(solution)/shard_map/ppermute | solution.py:414
  985.5 70.7 %collective-permute-start.9 = (bf16[256,1792]{1,0:T(8,128)(2,1)}, bf16[256,1792]{1,0:T(8,128)(2,1)}, u32[]{:S(2)}, u32[]{:S(2)}) collective-permute-start(bf16[256,1792]{1,0:T(8,128)(2,1)} %get-tuple-element.64), channel_id=1, source_target_pairs={{0,3},{1,2},{2,1},{3,0},{4,7},{5,6},{6,5},{7,4},{8,11},{9,10},{10,... | collective-permute-start | bytes 2752520 | tf_op jit(solution)/shard_map/ppermute | solution.py:414
  986.9 69.3 %copy-start.1 = (bf16[256,1792]{1,0:T(8,128)(2,1)}, bf16[256,1792]{1,0:T(8,128)(2,1)S(1)}, u32[]{:S(2)}) copy-start(bf16[256,1792]{1,0:T(8,128)(2,1)S(1)} %collective-permute-done.17.refs_10_) | copy-start | bytes 2752516
  986.9 69.3 %collective-permute-start.7 = (bf16[256,1792]{1,0:T(8,128)(2,1)}, bf16[256,1792]{1,0:T(8,128)(2,1)}, u32[]{:S(2)}, u32[]{:S(2)}) collective-permute-start(bf16[256,1792]{1,0:T(8,128)(2,1)} %get-tuple-element.65), channel_id=1, source_target_pairs={{0,2},{1,3},{2,0},{3,1},{4,6},{5,7},{6,4},{7,5},{8,10},{9,11},{10,... | collective-permute-start | bytes 2752520 | tf_op jit(solution)/shard_map/ppermute | solution.py:414
  (4 other events, 21.6 us)

commit v3 on v2

--- a/solution.py
+++ b/solution.py
@@ -12,9 +12,10 @@
 TAU_CLIP = 100.0
 ROPE_THETA = 50000.0
 TILE_N = 256
+OUT_N = 512
 CLIP_ROWS = 64
 LOG2_E = 1.4426950408889634
-VMEM_LIMIT = 62 * 1024 * 1024
+VMEM_LIMIT = 67043328
 
 
 def rope_tables(pos_ids):
@@ -121,8 +122,8 @@
 
     def weight_copy(w, at_tile):
         col0 = pl.multiple_of(core * half_cols + (tile0 + at_tile) * TILE_N, TILE_N)
-        w_hbm = (wq_hbm, wk_hbm, wv_hbm)[w]
-        return pltpu.make_async_copy(w_hbm.at[:, pl.ds(col0, TILE_N)], w_scr.at[w], w_sems.at[w])
+        w_hbm, slot = (wq_hbm, wk_hbm, wv_hbm)[w], lax.rem(at_tile, 2)
+        return pltpu.make_async_copy(w_hbm.at[:, pl.ds(col0, TILE_N)], w_scr.at[slot, w], w_sems.at[slot, w])
 
     @pl.when(jnp.logical_and(tile == 0, chunk == 0))
     def _():
@@ -147,13 +148,20 @@
         clip = ClipPass(tile * n_chunks + chunk, n_tiles * n_chunks, units, refs[2 * n_chunks + 5], *outs)
         clip.open()
 
+    @pl.when(chunk == 0)
+    def _():
+        @pl.when(tile + 1 < n_tiles)
+        def _():
+            for w in range(3):
+                weight_copy(w, tile + 1).start()
+
+        for w in range(3):
+            weight_copy(w, tile).wait()
+
+    slot = lax.rem(tile, 2)
+    x = x_scr[chunk]
     for w, o_ref in enumerate((q_ref, k_ref, v_ref)):
-
-        @pl.when(chunk == 0)
-        def _():
-            weight_copy(w, tile).wait()
-
-        acc = jnp.dot(x_scr[chunk], w_scr[w], preferred_element_type=jnp.float32)
+        acc = jnp.dot(x, w_scr[slot, w], preferred_element_type=jnp.float32)
         if w < 2:
             cos_t, sin_t = cos_ref[0], sin_ref[0]
             for h in range(TILE_N // HEAD_DIM):
@@ -166,10 +174,6 @@
             for u in range(len(clip.units)):
                 if min(u, 2) == w:
                     clip.scale(u)
-
-        @pl.when(jnp.logical_and(chunk == n_chunks - 1, tile + 1 < n_tiles))
-        def _():
-            weight_copy(w, tile + 1).start()
 
     if clip:
         clip.close()
@@ -190,8 +194,8 @@
     scratch = [
         pltpu.VMEM((n_chunks, 2 * rows, depth), jnp.bfloat16),
         pltpu.SemaphoreType.DMA((n_chunks, 2)),
-        pltpu.VMEM((3, depth, TILE_N), jnp.bfloat16),
-        pltpu.SemaphoreType.DMA((3,)),
+        pltpu.VMEM((2, 3, depth, TILE_N), jnp.bfloat16),
+        pltpu.SemaphoreType.DMA((2, 3)),
     ]
     clip_specs, clip_args, clip_outs = [], [], []
     if clip_cols:
@@ -327,7 +331,7 @@
         return [
             pltpu.make_async_copy(
                 o_scr.at[slot, pl.ds(c * rows, rows)],
-                o_hbm.at[idx_ref[1 + c], :, pl.ds(pl.multiple_of(at_tile * TILE_N, TILE_N), TILE_N)],
+                o_hbm.at[idx_ref[1 + c], :, pl.ds(pl.multiple_of(at_tile * OUT_N, OUT_N), OUT_N)],
                 o_sems.at[slot, c],
             )
             for c in range(n_chunks)
@@ -353,7 +357,10 @@
         for copy in out_copies(slot, tile - 2):
             copy.wait()
 
-    o_scr[slot] = jnp.dot(a_scr[...], wo_ref[...], preferred_element_type=jnp.float32).astype(o_scr.dtype)
+    a = a_scr[...]
+    for c0 in range(0, OUT_N, TILE_N):
+        cols = slice(c0, c0 + TILE_N)
+        o_scr[slot, :, cols] = jnp.dot(a, wo_ref[:, cols], preferred_element_type=jnp.float32).astype(o_scr.dtype)
     for u in range(len(clip.units)):
         clip.scale(u)
     for copy in out_copies(slot, tile):
@@ -373,9 +380,9 @@
     n_chunks = len(pieces) // (2 * n_groups)
     rows = pieces[0].shape[0]
     depth, width = w_o.shape
-    n_tiles = width // TILE_N
+    n_tiles = width // OUT_N
     any_spec = pl.BlockSpec(memory_space=pl.ANY)
-    tile_spec = pl.BlockSpec((depth, TILE_N), lambda n, idx: (0, n))
+    tile_spec = pl.BlockSpec((depth, OUT_N), lambda n, idx: (0, n))
     alias_at = 1 + len(pieces) + 3
     aliased, aliases = [clip_into], {alias_at: 1}
     if into is not None:
@@ -391,7 +398,7 @@
             out_specs=[any_spec, any_spec],
             scratch_shapes=[
                 pltpu.VMEM((n_chunks * rows, depth), jnp.bfloat16),
-                pltpu.VMEM((2, n_chunks * rows, TILE_N), jnp.bfloat16),
+                pltpu.VMEM((2, n_chunks * rows, OUT_N), jnp.bfloat16),
                 pltpu.SemaphoreType.DMA((len(pieces),)),
                 pltpu.SemaphoreType.DMA((2, n_chunks)),
             ]
@@ -441,9 +448,7 @@
             return project(index(*offsets), pieces, cos_t, sin_t, w_q, w_k, w_v, qkv, tile0, n_tiles, *clip)
 
         rest = tuple(range(1, n_chips))
-        split = half_tiles - max(half_tiles // 4, 1)
-        qkv = fill(None, (0,), 0, split)
-        qkv = fill(qkv, (0,), split, half_tiles - split)
+        qkv = fill(None, (0,), 0, half_tiles)
         qkv = fill(qkv, rest[:-1], *groups[0])
         qkv = fill(qkv, rest[-1:], *groups[0])
 
@@ -455,7 +460,8 @@
             vals, row_max = attend(*qkv, tile0 * heads_per_tile, n_group)
             local_max = jnp.max(row_max.reshape(n_group, -1), axis=1)
             spread = jnp.where(jnp.arange(2)[:, None] == core, local_max[None, :], -jnp.inf)
-            group_max = lax.pmax(spread, ("dp", "cp"))
+            every_max = lax.all_gather(spread, ("dp", "cp"))
+            group_max = jnp.max(every_max, axis=0)
             maxes.append(group_max)
             factor = jnp.where(group_max > TAU_CLIP, jnp.sqrt(TAU_CLIP / group_max), 1.0)
             factors.append(jnp.repeat(factor, HEAD_DIM, axis=1))

time: 1150 us -> 905 us (0.79)
  Pallas kernels: 804 us -> 602 us
  blocking collectives: 228 us -> 188 us
    pallas_call x5 -> x4, Pallas kernels: 552 us -> 355 us  [project(): pl.pallas_call(functools.partial(proj_kernel, n_chunks, n_alias, tile0, c...]
    pmax x2 -> x0, blocking collectives: 75.8 us -> none  [device_body(): group_max = lax.pmax(spread, ('dp', 'cp'))]
    all_gather x0 -> x2, blocking collectives: none -> 35.7 us  [device_body(): every_max = lax.all_gather(spread, ('dp', 'cp'))]
  transfers between devices with their start and end apart: 21 -> 21, of which waited for: 3 -> 3; matrix products, arithmetic and copies ran while one was open for 1% -> 2% of each run, Pallas kernels for 30% -> 26%
where the time goes in v3:
time: 905 us
  Pallas kernels  602 us (67%)
  blocking collectives  188 us (21%)
  waiting for transfers between devices  61.1 us (7%)
  local copies, waits for them, and re-layouts  21.8 us (2%)
  starting transfers between devices  20.1 us (2%)
  other arithmetic  10.4 us (1%)
    pallas_call x4, Pallas kernels, project(): pl.pallas_call(functools.partial(proj_kernel, n_chunks, n_alias, tile0, c...  355 us
    pallas_call x2, Pallas kernels, out_project(): pl.pallas_call(functools.partial(out_kernel, n_chunks, col_offs, len(alia...  155 us
    all_gather x1, blocking collectives, device_body(): all_pos = lax.all_gather(pos_ids, 'cp', tiled=True)  152 us
    pallas_call x2, Pallas kernels, attend(): pl.pallas_call(functools.partial(attn_kernel, blk), grid=(n_heads,), in_s...  92.7 us
    ppermute x21, waiting for transfers between devices, permute(): return lax.ppermute(x, 'cp', [(src, src ^ flip) for src in range(cp_size)])  61.1 us
    all_gather x2, blocking collectives, device_body(): every_max = lax.all_gather(spread, ('dp', 'cp'))  35.7 us
    ppermute x21, starting transfers between devices, permute(): return lax.ppermute(x, 'cp', [(src, src ^ flip) for src in range(cp_size)])  20.1 us
  transfers between devices with their start and end apart: 21, of which 3 were waited for; matrix products, arithmetic and copies ran while one was open for 2% of the time, Pallas kernels for 26%

profile of v3, /device:TPU:0, one launch (start us, length us, event | category | flops | bytes accessed | tf_op | source)
XLA Modules:
  0.0 904.8 jit_solution(14757717341336634579)
XLA Ops:
  0.7 9.2 %dynamic-slice_bitcast_fusion = (bf16[256,6656]{1,0:T(8,128)(2,1)S(1)}, bf16[256,6656]{1,0:T(8,128)(2,1)}, bf16[256,6656]{1,0:T(8,128)(2,1)}, bf16[256,6656]{1,0:T(8,128)(2,1)}) fusion(bf16[4,256,6656]{2,1,0:T(8,128)(2,1)} %param.6, s32[]{:T(128)S(6)} %select_n.93, s32[]{:T(128)S(6)} %select_n.91, s32[]{:T(128)S(6)} %select_n.90, s32[]{:T(128)S(6)} %select_n.92), kind=kLoop, calls=%fused_computation | loop fusion | bytes 27262992 | tf_op jit(solution)/shard_map/jit(dynamic_index_in_dim)/squeeze | solution.py:442
  9.9 3.2 collective-permute-start.2
  14.6 152.1 %all-gather = s32[8,1,256]{2,1,0:T(1,128)S(1)} all-gather(s32[1,1,256]{2,1,0:T(1,128)S(1)} %bitcast.63), channel_id=1, replica_groups=mesh['dp'=2,'cp'=8] {'cp'}, dimensions={0}, use_global_device_ids=true | all-gather | bytes 9216 | tf_op jit(solution)/shard_map/all_gather | solution.py:437
  169.4 3.7 fusion
  173.1 2.0 pad_maximum_fusion
  175.9 81.2 %shard_map.93 = (bf16[4,512,3328]{2,1,0:T(8,128)(2,1)}, bf16[4,512,3328]{2,1,0:T(8,128)(2,1)}, bf16[4,512,3328]{2,1,0:T(8,128)(2,1)}) custom-call(s32[2]{0:T(128)} %get-tuple-element.72.idx_ref, bf16[256,6656]{1,0:T(8,128)(2,1)} %copy-done, bf16[256,6656]{1,0:T(8,128)(2,1)} %collective-permute-done.6.refs_1_, ...), custom_call_target="tpu_custom_call" | custom-call | flops 68048388096 | bytes 139722752 | tf_op jit(solution)/shard_map/pallas_call | solution.py:206
  257.2 88.0 %shard_map.94 = (bf16[4,512,3328]{2,1,0:T(8,128)(2,1)}, bf16[4,512,3328]{2,1,0:T(8,128)(2,1)}, bf16[4,512,3328]{2,1,0:T(8,128)(2,1)}) custom-call(s32[3]{0:T(128)} %pad_add_fusion.2.idx_ref, bf16[256,6656]{1,0:T(8,128)(2,1)} %collective-permute-done.2.refs_0_, ...), custom_call_target="tpu_custom_call", output_to_operand_aliasing={{0}: (10, {}), {1}: (11, {}), {2}: (12, {})} | custom-call | flops 73282879488 | bytes 85196800 | tf_op jit(solution)/shard_map/pallas_call | solution.py:206
  345.2 47.7 %shard_map.95 = (bf16[4,512,3328]{2,1,0:T(8,128)(2,1)}, bf16[4,512,3328]{2,1,0:T(8,128)(2,1)}, bf16[4,512,3328]{2,1,0:T(8,128)(2,1)}) custom-call(s32[2]{0:T(128)} %get-tuple-element.71.idx_ref, bf16[256,6656]{1,0:T(8,128)(2,1)} %collective-permute-done.refs_0_.refs_4_, ...), custom_call_target="tpu_custom_call", output_to_operand_aliasing={{0}: (8, {}), {1}: (9, {}), {2}: (10, {})} | custom-call | flops 36641439744 | bytes 78381056 | tf_op jit(solution)/shard_map/pallas_call | solution.py:206
  392.9 49.7 %shard_map.96 = (bf16[4,512,1792]{2,1,0:T(8,128)(2,1)}, f32[112,128]{1,0:T(8,128)}) custom-call(bf16[4,512,3328]{2,1,0:T(8,128)(2,1)} %get-tuple-element.32.q_ref.refs_12_, bf16[4,512,3328]{2,1,0:T(8,128)(2,1)} %get-tuple-element.33.k_ref.refs_13_, bf16[4,512,3328]{2,1,0:T(8,128)(2,1)} %get-tuple-element.34.v_ref.refs_14_), custom_call_target="tpu_custom_call" | custom-call | flops 30064771072 | bytes 29360128 | tf_op jit(solution)/shard_map/pallas_call | solution.py:283
  444.5 11.7 %all_gather.12 = f32[16,2,14]{2,1,0:T(2,128)S(1)} all-gather(f32[1,2,14]{2,1,0:T(2,128)S(1)} %broadcast_select_fusion.1), channel_id=1, replica_groups=mesh['dp'=2,'cp'=8] {'dp','cp'}, dimensions={0}, use_global_device_ids=true | all-gather | bytes 1904 | tf_op jit(solution)/shard_map/all_gather | solution.py:463
  457.0 137.7 %shard_map.97 = (bf16[4,512,3328]{2,1,0:T(8,128)(2,1)}, bf16[4,512,3328]{2,1,0:T(8,128)(2,1)}, bf16[4,512,3328]{2,1,0:T(8,128)(2,1)}, bf16[6656,6656]{1,0:T(8,128)(2,1)}, bf16[6656,6656]{1,0:T(8,128)(2,1)}) custom-call(s32[4]{0:T(128)} %pad_add_fusion.idx_ref, ...), custom_call_target="tpu_custom_call", output_to_operand_aliasing={{0}: (13, {}), {1}: (14, {}), {2}: (15, {})} | custom-call | flops 94220845056 | bytes 81788928 | tf_op jit(solution)/shard_map/pallas_call | solution.py:206
  594.7 43.0 %shard_map.98 = (bf16[4,512,1536]{2,1,0:T(8,128)(2,1)}, f32[96,128]{1,0:T(8,128)}) custom-call(bf16[4,512,3328]{2,1,0:T(8,128)(2,1)} %get-tuple-element.37.q_ref, bf16[4,512,3328]{2,1,0:T(8,128)(2,1)} %get-tuple-element.38.k_ref, bf16[4,512,3328]{2,1,0:T(8,128)(2,1)} %get-tuple-element.39.v_ref), custom_call_target="tpu_custom_call" | custom-call | flops 25769803776 | bytes 25165824 | tf_op jit(solution)/shard_map/pallas_call | solution.py:283
  637.7 4.9 dynamic-slice_bitcast_fusion.12
  646.9 5.5 dynamic-slice_bitcast_fusion.4
  653.9 9.6 %collective-permute-done.18.refs_11_ = bf16[256,1536]{1,0:T(8,128)(2,1)} collective-permute-done((bf16[256,1536]{1,0:T(8,128)(2,1)S(1)}, bf16[256,1536]{1,0:T(8,128)(2,1)}, u32[]{:S(2)}, u32[]{:S(2)}) %collective-permute-start.18) | collective-permute-done | bytes 786464 | tf_op jit(solution)/shard_map/ppermute | solution.py:421
  663.5 1.6 collective-permute-start.12
  665.1 15.9 %collective-permute-done.16.refs_9_ = bf16[256,1536]{1,0:T(8,128)(2,1)} collective-permute-done((bf16[256,1536]{1,0:T(8,128)(2,1)S(1)}, bf16[256,1536]{1,0:T(8,128)(2,1)}, u32[]{:S(2)}, u32[]{:S(2)}) %collective-permute-start.16) | collective-permute-done | bytes 786464 | tf_op jit(solution)/shard_map/ppermute | solution.py:421
  681.6 35.5 %collective-permute-done.14.refs_7_ = bf16[256,1536]{1,0:T(8,128)(2,1)} collective-permute-done((bf16[256,1536]{1,0:T(8,128)(2,1)S(1)}, bf16[256,1536]{1,0:T(8,128)(2,1)}, u32[]{:S(2)}, u32[]{:S(2)}) %collective-permute-start.14) | collective-permute-done | bytes 786464 | tf_op jit(solution)/shard_map/ppermute | solution.py:421
  717.1 1.5 collective-permute-start.8
  719.1 24.0 %all_gather.13 = f32[16,2,12]{2,1,0:T(2,128)S(1)} all-gather(f32[1,2,12]{2,1,0:T(2,128)S(1)} %broadcast_select_fusion), channel_id=1, replica_groups=mesh['dp'=2,'cp'=8] {'dp','cp'}, dimensions={0}, use_global_device_ids=true | all-gather | bytes 1632 | tf_op jit(solution)/shard_map/all_gather | solution.py:463
  744.4 1.6 collective-permute-start.15
  746.2 1.6 collective-permute-start.11
  749.6 64.6 %shard_map.99 = (bf16[4,256,6656]{2,1,0:T(8,128)(2,1)}, bf16[6656,6656]{1,0:T(8,128)(2,1)}) custom-call(s32[2]{0:T(128)} %get-tuple-element.72.idx_ref, bf16[256,1792]{1,0:T(8,128)(2,1)} %get-tuple-element.53.refs_0_, bf16[256,1536]{1,0:T(8,128)(2,1)} %get-tuple-element.61.refs_1_, ...), custom_call_target="tpu_custom_call", output_to_operand_aliasing={{1}: (8, {})} | custom-call | flops 22682796032 | bytes 177209344 | tf_op jit(solution)/shard_map/pallas_call | solution.py:390
  814.2 90.3 %shard_map.100 = (bf16[4,256,6656]{2,1,0:T(8,128)(2,1)}, bf16[6656,6656]{1,0:T(8,128)(2,1)}) custom-call(s32[4]{0:T(128)} %pad_add_fusion.idx_ref, bf16[256,1792]{1,0:T(8,128)(2,1)} %collective-permute-done.7.refs_0_, bf16[256,1536]{1,0:T(8,128)(2,1)} %collective-permute-done.8.refs_1_, ...), custom_call_target="tpu_custom_call", output_to_operand_aliasing={{1}: (16, {}), {0}: (17, {})} | custom-call | flops 68048388096 | bytes 177209344 | tf_op jit(solution)/shard_map/pallas_call | solution.py:390
  (77 shorter events, 17.6 us)
Async XLA Ops:
  9.9 165.1 %collective-permute-start.2 = (bf16[256,6656]{1,0:T(8,128)(2,1)}, bf16[256,6656]{1,0:T(8,128)(2,1)}, u32[]{:S(2)}, u32[]{:S(2)}) collective-permute-start(bf16[256,6656]{1,0:T(8,128)(2,1)} %get-tuple-element.49), channel_id=1, source_target_pairs={{0,2},{1,3},{2,0},{3,1},{4,6},{5,7},{6,4},{7,5},{8,10},{9,11},{10,... | collective-permute-start | bytes 10223624 | tf_op jit(solution)/shard_map/ppermute | solution.py:421
  13.1 162.3 %collective-permute-start = (bf16[256,6656]{1,0:T(8,128)(2,1)}, bf16[256,6656]{1,0:T(8,128)(2,1)}, u32[]{:S(2)}, u32[]{:S(2)}) collective-permute-start(bf16[256,6656]{1,0:T(8,128)(2,1)} %get-tuple-element.50), channel_id=1, source_target_pairs={{0,6},{1,7},{2,4},{3,5},{4,2},{5,3},{6,0},{7,1},{8,14},{9,15},{10,... | collective-permute-start | bytes 10223624 | tf_op jit(solution)/shard_map/ppermute | solution.py:421
  14.6 161.0 %collective-permute-start.4 = (bf16[256,6656]{1,0:T(8,128)(2,1)}, bf16[256,6656]{1,0:T(8,128)(2,1)}, u32[]{:S(2)}, u32[]{:S(2)}) collective-permute-start(bf16[256,6656]{1,0:T(8,128)(2,1)} %get-tuple-element.51), channel_id=1, source_target_pairs={{0,4},{1,5},{2,6},{3,7},{4,0},{5,1},{6,2},{7,3},{8,12},{9,13},{10,... | collective-permute-start | bytes 10223624 | tf_op jit(solution)/shard_map/ppermute | solution.py:421
  14.6 161.3 %collective-permute-start.6 = (bf16[256,6656]{1,0:T(8,128)(2,1)S(1)}, bf16[256,6656]{1,0:T(8,128)(2,1)}, u32[]{:S(2)}, u32[]{:S(2)}) collective-permute-start(bf16[256,6656]{1,0:T(8,128)(2,1)S(1)} %get-tuple-element.48.refs_0_), channel_id=1, source_target_pairs={{0,1},{1,0},{2,3},{3,2},{4,5},{5,4},{6,7},{7,6},{8,9},{9,8},{10,11... | collective-permute-start | bytes 10223624 | tf_op jit(solution)/shard_map/ppermute | solution.py:421
  175.0 82.1 %collective-permute-start.3 = (bf16[256,6656]{1,0:T(8,128)(2,1)}, bf16[256,6656]{1,0:T(8,128)(2,1)}, u32[]{:S(2)}, u32[]{:S(2)}) collective-permute-start(bf16[256,6656]{1,0:T(8,128)(2,1)} %collective-permute-done.2.refs_0_), channel_id=1, source_target_pairs={{0,1},{1,0},{2,3},{3,2},{4,5},{5,4},{6,7},{7,6},{8,9},{9,8},{10,11... | collective-permute-start | bytes 10223624 | tf_op jit(solution)/shard_map/ppermute | solution.py:421
  175.4 169.8 %collective-permute-start.1 = (bf16[256,6656]{1,0:T(8,128)(2,1)}, bf16[256,6656]{1,0:T(8,128)(2,1)}, u32[]{:S(2)}, u32[]{:S(2)}) collective-permute-start(bf16[256,6656]{1,0:T(8,128)(2,1)} %collective-permute-done.refs_0_.refs_4_), channel_id=1, source_target_pairs={{0,1},{1,0},{2,3},{3,2},{4,5},{5,4},{6,7},{7,6},{8,9},{9,8},{10,11... | collective-permute-start | bytes 10223624 | tf_op jit(solution)/shard_map/ppermute | solution.py:421
  175.6 81.6 %collective-permute-start.5 = (bf16[256,6656]{1,0:T(8,128)(2,1)}, bf16[256,6656]{1,0:T(8,128)(2,1)}, u32[]{:S(2)}, u32[]{:S(2)}) collective-permute-start(bf16[256,6656]{1,0:T(8,128)(2,1)} %collective-permute-done.4.refs_2_), channel_id=1, source_target_pairs={{0,1},{1,0},{2,3},{3,2},{4,5},{5,4},{6,7},{7,6},{8,9},{9,8},{10,11... | collective-permute-start | bytes 10223624 | tf_op jit(solution)/shard_map/ppermute | solution.py:421
  637.7 81.0 %copy-start.4 = (f32[96,128]{1,0:T(8,128)S(1)}, f32[96,128]{1,0:T(8,128)}, u32[]{:S(2)}) copy-start(f32[96,128]{1,0:T(8,128)} %get-tuple-element.41) | copy-start | bytes 147460
  637.7 81.3 %copy-start.7 = (pred[2]{0:T(512)(128)(4,1)S(1)}, pred[2]{0:T(512)(128)(4,1)}, u32[]{:S(2)}) copy-start(pred[2]{0:T(512)(128)(4,1)} %iota_compare_fusion) | copy-start | bytes 10
  637.7 105.4 %copy-start.6 = (f32[2,14]{1,0:T(2,128)S(1)}, f32[2,14]{1,0:T(2,128)}, u32[]{:S(2)}) copy-start(f32[2,14]{1,0:T(2,128)} %copy-done.5) | copy-start | bytes 340
  642.6 10.3 %collective-permute-start.20 = (bf16[256,1536]{1,0:T(8,128)(2,1)S(1)}, bf16[256,1536]{1,0:T(8,128)(2,1)S(1)}, u32[]{:S(2)}, u32[]{:S(2)}) collective-permute-start(bf16[256,1536]{1,0:T(8,128)(2,1)S(1)} %get-tuple-element.60), channel_id=1, source_target_pairs={{0,1},{1,0},{2,3},{3,2},{4,5},{5,4},{6,7},{7,6},{8,9},{9,8},{10,11... | collective-permute-start | bytes 2359304 | tf_op jit(solution)/shard_map/ppermute | solution.py:421
  642.9 20.6 %collective-permute-start.18 = (bf16[256,1536]{1,0:T(8,128)(2,1)S(1)}, bf16[256,1536]{1,0:T(8,128)(2,1)}, u32[]{:S(2)}, u32[]{:S(2)}) collective-permute-start(bf16[256,1536]{1,0:T(8,128)(2,1)S(1)} %get-tuple-element.62), channel_id=1, source_target_pairs={{0,7},{1,6},{2,5},{3,4},{4,3},{5,2},{6,1},{7,0},{8,15},{9,14},{10,... | collective-permute-start | bytes 2359304 | tf_op jit(solution)/shard_map/ppermute | solution.py:421
  644.2 36.9 %collective-permute-start.16 = (bf16[256,1536]{1,0:T(8,128)(2,1)S(1)}, bf16[256,1536]{1,0:T(8,128)(2,1)}, u32[]{:S(2)}, u32[]{:S(2)}) collective-permute-start(bf16[256,1536]{1,0:T(8,128)(2,1)S(1)} %get-tuple-element.63), channel_id=1, source_target_pairs={{0,6},{1,7},{2,4},{3,5},{4,2},{5,3},{6,0},{7,1},{8,14},{9,15},{10,... | collective-permute-start | bytes 2359304 | tf_op jit(solution)/shard_map/ppermute | solution.py:421
  645.6 71.5 %collective-permute-start.14 = (bf16[256,1536]{1,0:T(8,128)(2,1)S(1)}, bf16[256,1536]{1,0:T(8,128)(2,1)}, u32[]{:S(2)}, u32[]{:S(2)}) collective-permute-start(bf16[256,1536]{1,0:T(8,128)(2,1)S(1)} %get-tuple-element.64), channel_id=1, source_target_pairs={{0,5},{1,4},{2,7},{3,6},{4,1},{5,0},{6,3},{7,2},{8,13},{9,12},{10,... | collective-permute-start | bytes 2359304 | tf_op jit(solution)/shard_map/ppermute | solution.py:421
  652.4 95.3 %collective-permute-start.19 = (bf16[256,1792]{1,0:T(8,128)(2,1)S(1)}, bf16[256,1792]{1,0:T(8,128)(2,1)}, u32[]{:S(2)}, u32[]{:S(2)}) collective-permute-start(bf16[256,1792]{1,0:T(8,128)(2,1)S(1)} %get-tuple-element.52), channel_id=1, source_target_pairs={{0,1},{1,0},{2,3},{3,2},{4,5},{5,4},{6,7},{7,6},{8,9},{9,8},{10,11... | collective-permute-start | bytes 2752520 | tf_op jit(solution)/shard_map/ppermute | solution.py:421
  652.8 96.2 %collective-permute-start.17 = (bf16[256,1792]{1,0:T(8,128)(2,1)S(1)}, bf16[256,1792]{1,0:T(8,128)(2,1)}, u32[]{:S(2)}, u32[]{:S(2)}) collective-permute-start(bf16[256,1792]{1,0:T(8,128)(2,1)S(1)} %get-tuple-element.54), channel_id=1, source_target_pairs={{0,7},{1,6},{2,5},{3,4},{4,3},{5,2},{6,1},{7,0},{8,15},{9,14},{10,... | collective-permute-start | bytes 2752520 | tf_op jit(solution)/shard_map/ppermute | solution.py:421
  663.5 80.9 %collective-permute-start.12 = (bf16[256,1536]{1,0:T(8,128)(2,1)}, bf16[256,1536]{1,0:T(8,128)(2,1)S(1)}, u32[]{:S(2)}, u32[]{:S(2)}) collective-permute-start(bf16[256,1536]{1,0:T(8,128)(2,1)} %get-tuple-element.65), channel_id=1, source_target_pairs={{0,4},{1,5},{2,6},{3,7},{4,0},{5,1},{6,2},{7,3},{8,12},{9,13},{10,... | collective-permute-start | bytes 2359304 | tf_op jit(solution)/shard_map/ppermute | solution.py:421
  681.1 64.9 %collective-permute-start.10 = (bf16[256,1536]{1,0:T(8,128)(2,1)}, bf16[256,1536]{1,0:T(8,128)(2,1)S(1)}, u32[]{:S(2)}, u32[]{:S(2)}) collective-permute-start(bf16[256,1536]{1,0:T(8,128)(2,1)} %get-tuple-element.66), channel_id=1, source_target_pairs={{0,3},{1,2},{2,1},{3,0},{4,7},{5,6},{6,5},{7,4},{8,11},{9,10},{10,... | collective-permute-start | bytes 2359304 | tf_op jit(solution)/shard_map/ppermute | solution.py:421
  717.1 29.0 %collective-permute-start.8 = (bf16[256,1536]{1,0:T(8,128)(2,1)}, bf16[256,1536]{1,0:T(8,128)(2,1)}, u32[]{:S(2)}, u32[]{:S(2)}) collective-permute-start(bf16[256,1536]{1,0:T(8,128)(2,1)} %get-tuple-element.67), channel_id=1, source_target_pairs={{0,2},{1,3},{2,0},{3,1},{4,6},{5,7},{6,4},{7,5},{8,10},{9,11},{10,... | collective-permute-start | bytes 2359304 | tf_op jit(solution)/shard_map/ppermute | solution.py:421
  744.4 69.8 %collective-permute-start.15 = (bf16[256,1792]{1,0:T(8,128)(2,1)}, bf16[256,1792]{1,0:T(8,128)(2,1)}, u32[]{:S(2)}, u32[]{:S(2)}) collective-permute-start(bf16[256,1792]{1,0:T(8,128)(2,1)} %get-tuple-element.55), channel_id=1, source_target_pairs={{0,6},{1,7},{2,4},{3,5},{4,2},{5,3},{6,0},{7,1},{8,14},{9,15},{10,... | collective-permute-start | bytes 2752520 | tf_op jit(solution)/shard_map/ppermute | solution.py:421
  746.0 68.2 %collective-permute-start.13 = (bf16[256,1792]{1,0:T(8,128)(2,1)}, bf16[256,1792]{1,0:T(8,128)(2,1)}, u32[]{:S(2)}, u32[]{:S(2)}) collective-permute-start(bf16[256,1792]{1,0:T(8,128)(2,1)} %get-tuple-element.56), channel_id=1, source_target_pairs={{0,5},{1,4},{2,7},{3,6},{4,1},{5,0},{6,3},{7,2},{8,13},{9,12},{10,... | collective-permute-start | bytes 2752520 | tf_op jit(solution)/shard_map/ppermute | solution.py:421
  746.2 68.1 %collective-permute-start.11 = (bf16[256,1792]{1,0:T(8,128)(2,1)}, bf16[256,1792]{1,0:T(8,128)(2,1)}, u32[]{:S(2)}, u32[]{:S(2)}) collective-permute-start(bf16[256,1792]{1,0:T(8,128)(2,1)} %get-tuple-element.57), channel_id=1, source_target_pairs={{0,4},{1,5},{2,6},{3,7},{4,0},{5,1},{6,2},{7,3},{8,12},{9,13},{10,... | collective-permute-start | bytes 2752520 | tf_op jit(solution)/shard_map/ppermute | solution.py:421
  747.7 66.5 %collective-permute-start.9 = (bf16[256,1792]{1,0:T(8,128)(2,1)}, bf16[256,1792]{1,0:T(8,128)(2,1)}, u32[]{:S(2)}, u32[]{:S(2)}) collective-permute-start(bf16[256,1792]{1,0:T(8,128)(2,1)} %get-tuple-element.58), channel_id=1, source_target_pairs={{0,3},{1,2},{2,1},{3,0},{4,7},{5,6},{6,5},{7,4},{8,11},{9,10},{10,... | collective-permute-start | bytes 2752520 | tf_op jit(solution)/shard_map/ppermute | solution.py:421
  749.0 65.2 %collective-permute-start.7 = (bf16[256,1792]{1,0:T(8,128)(2,1)}, bf16[256,1792]{1,0:T(8,128)(2,1)}, u32[]{:S(2)}, u32[]{:S(2)}) collective-permute-start(bf16[256,1792]{1,0:T(8,128)(2,1)} %get-tuple-element.59), channel_id=1, source_target_pairs={{0,2},{1,3},{2,0},{3,1},{4,6},{5,7},{6,4},{7,5},{8,10},{9,11},{10,... | collective-permute-start | bytes 2752520 | tf_op jit(solution)/shard_map/ppermute | solution.py:421
  (6 other events, 28.1 us)

commit v4 on v3

--- a/solution.py
+++ b/solution.py
@@ -13,6 +13,7 @@
 ROPE_THETA = 50000.0
 TILE_N = 256
 OUT_N = 512
+SPLIT = 2
 CLIP_ROWS = 64
 LOG2_E = 1.4426950408889634
 VMEM_LIMIT = 67043328
@@ -114,33 +115,43 @@
     core = idx_ref[0]
     half_cols = wq_hbm.shape[1] // 2
 
-    def piece_copy(c, side):
-        row0 = (core if side == 0 else 1 - core) * rows
-        return pltpu.make_async_copy(
-            pieces[2 * c + side], x_scr.at[c, pl.ds(pl.multiple_of(row0, rows), rows)], x_sems.at[c, side]
-        )
-
-    def weight_copy(w, at_tile):
+    def piece_copies(c):
+        part = rows // SPLIT
+        for side in range(2):
+            for n in range(SPLIT):
+                row0 = (core if side == 0 else 1 - core) * rows + n * part
+                yield pltpu.make_async_copy(
+                    pieces[2 * c + side].at[pl.ds(n * part, part)],
+                    x_scr.at[c, pl.ds(pl.multiple_of(row0, part), part)],
+                    x_sems.at[c, side, n],
+                )
+
+    def weight_copies(at_tile):
         col0 = pl.multiple_of(core * half_cols + (tile0 + at_tile) * TILE_N, TILE_N)
-        w_hbm, slot = (wq_hbm, wk_hbm, wv_hbm)[w], lax.rem(at_tile, 2)
-        return pltpu.make_async_copy(w_hbm.at[:, pl.ds(col0, TILE_N)], w_scr.at[slot, w], w_sems.at[slot, w])
+        slot, part = lax.rem(at_tile, 2), wq_hbm.shape[0] // SPLIT
+        for w, w_hbm in enumerate((wq_hbm, wk_hbm, wv_hbm)):
+            for n in range(SPLIT):
+                at = pl.ds(n * part, part)
+                yield pltpu.make_async_copy(
+                    w_hbm.at[at, pl.ds(col0, TILE_N)], w_scr.at[slot, w, at], w_sems.at[slot, w, n]
+                )
 
     @pl.when(jnp.logical_and(tile == 0, chunk == 0))
     def _():
-        for side in range(2):
-            piece_copy(0, side).start()
-        for w in range(3):
-            weight_copy(w, 0).start()
+        for copy in piece_copies(0):
+            copy.start()
+        for copy in weight_copies(0):
+            copy.start()
         for c in range(1, n_chunks):
-            for side in range(2):
-                piece_copy(c, side).start()
+            for copy in piece_copies(c):
+                copy.start()
 
     for c in range(n_chunks):
 
         @pl.when(jnp.logical_and(tile == 0, chunk == c))
         def _():
-            for side in range(2):
-                piece_copy(c, side).wait()
+            for copy in piece_copies(c):
+                copy.wait()
 
     clip = None
     if clip_cols:
@@ -152,11 +163,11 @@
     def _():
         @pl.when(tile + 1 < n_tiles)
         def _():
-            for w in range(3):
-                weight_copy(w, tile + 1).start()
-
-        for w in range(3):
-            weight_copy(w, tile).wait()
+            for copy in weight_copies(tile + 1):
+                copy.start()
+
+        for copy in weight_copies(tile):
+            copy.wait()
 
     slot = lax.rem(tile, 2)
     x = x_scr[chunk]
@@ -193,9 +204,9 @@
     first_alias = 1 + 2 * n_chunks + 5 + (1 if clip_cols else 0)
     scratch = [
         pltpu.VMEM((n_chunks, 2 * rows, depth), jnp.bfloat16),
-        pltpu.SemaphoreType.DMA((n_chunks, 2)),
+        pltpu.SemaphoreType.DMA((n_chunks, 2, SPLIT)),
         pltpu.VMEM((2, 3, depth, TILE_N), jnp.bfloat16),
-        pltpu.SemaphoreType.DMA((2, 3)),
+        pltpu.SemaphoreType.DMA((2, 3, SPLIT)),
     ]
     clip_specs, clip_args, clip_outs = [], [], []
     if clip_cols:
@@ -223,7 +234,8 @@
     )(idx, *pieces, cos_t, sin_t, w_q, w_k, w_v, *clip_args, *(into or ()))
 
 
-def attn_kernel(blk, q_ref, k_ref, v_ref, o_ref, m_ref, s_scr, p_scr):
+def attn_kernel(blk, rank_ref, q_ref, k_ref, v_ref, *refs):
+    *o_refs, m_ref, s_scr, p_scr, o_scr = refs
     n_chunks, rows, _ = q_ref.shape
     per_chunk = rows // blk
     n_blocks = n_chunks * per_chunk
@@ -267,36 +279,43 @@
         values = v_ref[...].reshape(n_chunks * rows, HEAD_DIM)[:keys]
         acc = jnp.dot(p_scr[i % 2, :, :keys], values, preferred_element_type=jnp.float32)
         row_sum = jnp.sum(lane_sum, axis=-1, keepdims=True)
-        r0 = (i % per_chunk) * blk
-        o_ref[i // per_chunk, r0 : r0 + blk, :] = (acc / row_sum).astype(o_ref.dtype)
+        o_scr[i] = (acc / row_sum).astype(o_scr.dtype)
         if i + 1 < n_blocks:
             row_max = next_max
+    for flip, o_ref in enumerate(o_refs):
+        o_ref[...] = o_scr[lax.bitwise_xor(rank_ref[0], flip)]
     m_ref[...] = jnp.broadcast_to(jnp.max(head_max, axis=0, keepdims=True) * scale, m_ref.shape)
 
 
-def attend(q, k, v, head0, n_heads):
+def attend(rank, q, k, v, head0, n_heads):
     n_chunks, rows, _ = q.shape
-    blk = min(256, rows)
-    in_spec = pl.BlockSpec((n_chunks, rows, HEAD_DIM), lambda h: (0, 0, head0 + h))
-    o_spec = pl.BlockSpec((n_chunks, rows, HEAD_DIM), lambda h: (0, 0, h))
+    blk = rows // 2
+    n_blocks = 2 * n_chunks
     seq = n_chunks * rows
+    in_spec = pl.BlockSpec((n_chunks, rows, HEAD_DIM), lambda h, rank: (0, 0, head0 + h))
+    o_spec = pl.BlockSpec((blk, HEAD_DIM), lambda h, rank: (0, h))
     return pl.pallas_call(
         functools.partial(attn_kernel, blk),
-        grid=(n_heads,),
-        in_specs=[in_spec] * 3,
-        out_specs=[o_spec, pl.BlockSpec((8, HEAD_DIM), lambda h: (h, 0))],
-        out_shape=[
-            jax.ShapeDtypeStruct((n_chunks, rows, n_heads * HEAD_DIM), jnp.bfloat16),
-            jax.ShapeDtypeStruct((8 * n_heads, HEAD_DIM), jnp.float32),
-        ],
-        scratch_shapes=[pltpu.VMEM((2, blk, seq), jnp.float32), pltpu.VMEM((2, blk, seq), jnp.bfloat16)],
+        grid_spec=pltpu.PrefetchScalarGridSpec(
+            num_scalar_prefetch=1,
+            grid=(n_heads,),
+            in_specs=[in_spec] * 3,
+            out_specs=[o_spec] * n_blocks + [pl.BlockSpec((8, HEAD_DIM), lambda h, rank: (h, 0))],
+            scratch_shapes=[
+                pltpu.VMEM((2, blk, seq), jnp.float32),
+                pltpu.VMEM((2, blk, seq), jnp.bfloat16),
+                pltpu.VMEM((n_blocks, blk, HEAD_DIM), jnp.bfloat16),
+            ],
+        ),
+        out_shape=[jax.ShapeDtypeStruct((blk, n_heads * HEAD_DIM), jnp.bfloat16)] * n_blocks
+        + [jax.ShapeDtypeStruct((8 * n_heads, HEAD_DIM), jnp.float32)],
         compiler_params=pltpu.CompilerParams(dimension_semantics=("arbitrary",), vmem_limit_bytes=VMEM_LIMIT),
         cost_estimate=pl.CostEstimate(
             flops=8 * seq * seq * HEAD_DIM * n_heads // 2,
             bytes_accessed=8 * seq * HEAD_DIM * n_heads,
             transcendentals=seq * seq * n_heads // 2,
         ),
-    )(q, k, v)
+    )(rank, q, k, v)
 
 
 def out_kernel(n_chunks, col_offs, n_alias, clip_cols, idx_ref, *refs):
@@ -457,7 +476,7 @@
             n_group = n_tiles * heads_per_tile
             if g == 1:
                 *qkv, w_q_new, w_k_new = fill(qkv, rest, tile0, n_tiles, clip_cols[0], factors[0])
-            vals, row_max = attend(*qkv, tile0 * heads_per_tile, n_group)
+            *vals, row_max = attend(cp_rank.astype(jnp.int32)[None], *qkv, tile0 * heads_per_tile, n_group)
             local_max = jnp.max(row_max.reshape(n_group, -1), axis=1)
             spread = jnp.where(jnp.arange(2)[:, None] == core, local_max[None, :], -jnp.inf)
             every_max = lax.all_gather(spread, ("dp", "cp"))
@@ -466,12 +485,10 @@
             factor = jnp.where(group_max > TAU_CLIP, jnp.sqrt(TAU_CLIP / group_max), 1.0)
             factors.append(jnp.repeat(factor, HEAD_DIM, axis=1))
             clip_cols.append(tuple((h * half_tiles + tile0) * TILE_N for h in range(2)))
-            vals = vals.reshape(cp_size, -1, vals.shape[-1])
             got = {}
-            for d in range(n_chips):
-                for side in range(2):
-                    piece = lax.dynamic_index_in_dim(vals, cp_rank ^ (2 * d + side), 0, keepdims=False)
-                    got[d, side] = permute(piece, 2 * d + side) if d or side else piece
+            for flip, piece in enumerate(vals):
+                at = divmod(flip, 2)
+                got[at] = permute(piece, flip) if flip else piece
             sent.append(got)
         head_max = jnp.concatenate(maxes, axis=1).reshape(n_heads)
 

time: 905 us -> 910 us (level)
  blocking collectives: 188 us -> 217 us
  waiting for transfers between devices: 61.1 us -> 43.5 us
  local copies, waits for them, and re-layouts: 21.8 us -> 11.4 us
    all_gather x2, blocking collectives: 35.7 us -> 65.1 us  [device_body(): every_max = lax.all_gather(spread, ('dp', 'cp'))]
    ppermute x21, waiting for transfers between devices: 61.1 us -> 43.5 us  [permute(): return lax.ppermute(x, 'cp', [(src, src ^ flip) for src in range(cp_size)])]
    squeeze x2 -> x0, local copies, waits for them, and re-layouts: 10.4 us -> none  [device_body(): lax.dynamic_index_in_dim(vals, cp_rank ^ 2 * d + side, 0, keepdims=False)]
  transfers between devices with their start and end apart: 21 -> 21, of which waited for: 3 -> 3; matrix products, arithmetic and copies ran while one was open for 2% -> 1% of each run, Pallas kernels for 26% -> 26%
where the time goes in v4:
time: 910 us
  Pallas kernels  605 us (66%)
  blocking collectives  217 us (24%)
  waiting for transfers between devices  43.5 us (5%)
  starting transfers between devices  18.9 us (2%)
  other arithmetic  12.4 us (1%)
  local copies, waits for them, and re-layouts  11.4 us (1%)
    pallas_call x4, Pallas kernels, project(): pl.pallas_call(functools.partial(proj_kernel, n_chunks, n_alias, tile0, c...  356 us
    pallas_call x2, Pallas kernels, out_project(): pl.pallas_call(functools.partial(out_kernel, n_chunks, col_offs, len(alia...  155 us
    all_gather x1, blocking collectives, device_body(): all_pos = lax.all_gather(pos_ids, 'cp', tiled=True)  152 us
    pallas_call x2, Pallas kernels, attend(): pl.pallas_call(functools.partial(attn_kernel, blk), grid_spec=pltpu.Prefe...  94.3 us
    all_gather x2, blocking collectives, device_body(): every_max = lax.all_gather(spread, ('dp', 'cp'))  65.1 us
    ppermute x21, waiting for transfers between devices, permute(): return lax.ppermute(x, 'cp', [(src, src ^ flip) for src in range(cp_size)])  43.5 us
    ppermute x21, starting transfers between devices, permute(): return lax.ppermute(x, 'cp', [(src, src ^ flip) for src in range(cp_size)])  18.9 us
  transfers between devices with their start and end apart: 21, of which 3 were waited for; matrix products, arithmetic and copies ran while one was open for 1% of the time, Pallas kernels for 26%

profile of v4, /device:TPU:0, one launch (start us, length us, event | category | flops | bytes accessed | tf_op | source)
XLA Modules:
  0.0 909.8 jit_solution(10757246111970473425)
XLA Ops:
  0.7 9.2 %dynamic-slice_bitcast_fusion = (bf16[256,6656]{1,0:T(8,128)(2,1)S(1)}, bf16[256,6656]{1,0:T(8,128)(2,1)}, bf16[256,6656]{1,0:T(8,128)(2,1)}, bf16[256,6656]{1,0:T(8,128)(2,1)}) fusion(bf16[4,256,6656]{2,1,0:T(8,128)(2,1)} %param.6, s32[]{:T(128)S(6)} %select_n.59, s32[]{:T(128)S(6)} %select_n.57, s32[]{:T(128)S(6)} %select_n.56, s32[]{:T(128)S(6)} %select_n.58), kind=kLoop, calls=%fused_computation | loop fusion | bytes 27262992 | tf_op jit(solution)/shard_map/jit(dynamic_index_in_dim)/squeeze | solution.py:461
  9.9 3.2 collective-permute-start.2
  13.1 1.5 collective-permute-start
  14.6 152.2 %all-gather = s32[8,1,256]{2,1,0:T(1,128)S(1)} all-gather(s32[1,1,256]{2,1,0:T(1,128)S(1)} %bitcast.28), channel_id=1, replica_groups=mesh['dp'=2,'cp'=8] {'cp'}, dimensions={0}, use_global_device_ids=true | all-gather | bytes 9216 | tf_op jit(solution)/shard_map/all_gather | solution.py:456
  169.3 3.7 fusion
  173.0 2.0 pad_maximum_fusion
  175.9 81.6 %shard_map.93 = (bf16[4,512,3328]{2,1,0:T(8,128)(2,1)}, bf16[4,512,3328]{2,1,0:T(8,128)(2,1)}, bf16[4,512,3328]{2,1,0:T(8,128)(2,1)}) custom-call(s32[2]{0:T(128)} %get-tuple-element.84.idx_ref, bf16[256,6656]{1,0:T(8,128)(2,1)} %copy-done, bf16[256,6656]{1,0:T(8,128)(2,1)} %collective-permute-done.6.refs_1_, ...), custom_call_target="tpu_custom_call" | custom-call | flops 68048388096 | bytes 139722752 | tf_op jit(solution)/shard_map/pallas_call | solution.py:217
  257.5 88.5 %shard_map.94 = (bf16[4,512,3328]{2,1,0:T(8,128)(2,1)}, bf16[4,512,3328]{2,1,0:T(8,128)(2,1)}, bf16[4,512,3328]{2,1,0:T(8,128)(2,1)}) custom-call(s32[3]{0:T(128)} %pad_add_fusion.2.idx_ref, bf16[256,6656]{1,0:T(8,128)(2,1)} %collective-permute-done.2.refs_0_, ...), custom_call_target="tpu_custom_call", output_to_operand_aliasing={{0}: (10, {}), {1}: (11, {}), {2}: (12, {})} | custom-call | flops 73282879488 | bytes 85196800 | tf_op jit(solution)/shard_map/pallas_call | solution.py:217
  346.0 47.9 %shard_map.95 = (bf16[4,512,3328]{2,1,0:T(8,128)(2,1)}, bf16[4,512,3328]{2,1,0:T(8,128)(2,1)}, bf16[4,512,3328]{2,1,0:T(8,128)(2,1)}) custom-call(s32[2]{0:T(128)} %get-tuple-element.83.idx_ref, bf16[256,6656]{1,0:T(8,128)(2,1)} %collective-permute-done.refs_0_.refs_4_, ...), custom_call_target="tpu_custom_call", output_to_operand_aliasing={{0}: (8, {}), {1}: (9, {}), {2}: (10, {})} | custom-call | flops 36641439744 | bytes 78381056 | tf_op jit(solution)/shard_map/pallas_call | solution.py:217
  393.9 50.7 %shard_map.96 = (bf16[256,1792]{1,0:T(8,128)(2,1)}, bf16[256,1792]{1,0:T(8,128)(2,1)}, bf16[256,1792]{1,0:T(8,128)(2,1)}, bf16[256,1792]{1,0:T(8,128)(2,1)}, bf1...) custom-call(s32[1]{0:T(128)} %bitcast.4.rank_ref, ...), custom_call_target="tpu_custom_call" | custom-call | flops 30064771072 | bytes 29360128 | tf_op jit(solution)/shard_map/pallas_call | solution.py:297
  446.4 11.7 %all_gather.12 = f32[16,2,14]{2,1,0:T(2,128)S(1)} all-gather(f32[1,2,14]{2,1,0:T(2,128)S(1)} %broadcast_select_fusion.1), channel_id=1, replica_groups=mesh['dp'=2,'cp'=8] {'dp','cp'}, dimensions={0}, use_global_device_ids=true | all-gather | bytes 1904 | tf_op jit(solution)/shard_map/all_gather | solution.py:482
  458.8 138.2 %shard_map.97 = (bf16[4,512,3328]{2,1,0:T(8,128)(2,1)}, bf16[4,512,3328]{2,1,0:T(8,128)(2,1)}, bf16[4,512,3328]{2,1,0:T(8,128)(2,1)}, bf16[6656,6656]{1,0:T(8,128)(2,1)}, bf16[6656,6656]{1,0:T(8,128)(2,1)}) custom-call(s32[4]{0:T(128)} %pad_add_fusion.idx_ref, ...), custom_call_target="tpu_custom_call", output_to_operand_aliasing={{0}: (13, {}), {1}: (14, {}), {2}: (15, {})} | custom-call | flops 94220845056 | bytes 81788928 | tf_op jit(solution)/shard_map/pallas_call | solution.py:217
  597.0 43.7 %shard_map.98 = (bf16[256,1536]{1,0:T(8,128)(2,1)}, bf16[256,1536]{1,0:T(8,128)(2,1)}, bf16[256,1536]{1,0:T(8,128)(2,1)}, bf16[256,1536]{1,0:T(8,128)(2,1)}, bf1...) custom-call(s32[1]{0:T(128)} %bitcast.4.rank_ref, ...), custom_call_target="tpu_custom_call" | custom-call | flops 25769803776 | bytes 25165824 | tf_op jit(solution)/shard_map/pallas_call | solution.py:297
  640.6 1.6 collective-permute-start.8
  642.4 1.6 collective-permute-start.12
  644.1 1.6 collective-permute-start.7
  645.7 15.7 %collective-permute-done.8.refs_1_ = bf16[256,1536]{1,0:T(8,128)(2,1)} collective-permute-done((bf16[256,1536]{1,0:T(8,128)(2,1)}, bf16[256,1536]{1,0:T(8,128)(2,1)}, u32[]{:S(2)}, u32[]{:S(2)}) %collective-permute-start.8) | collective-permute-done | bytes 786464 | tf_op jit(solution)/shard_map/ppermute | solution.py:440
  661.4 15.9 %collective-permute-done.10.refs_3_ = bf16[256,1536]{1,0:T(8,128)(2,1)} collective-permute-done((bf16[256,1536]{1,0:T(8,128)(2,1)}, bf16[256,1536]{1,0:T(8,128)(2,1)}, u32[]{:S(2)}, u32[]{:S(2)}) %collective-permute-start.10) | collective-permute-done | bytes 786464 | tf_op jit(solution)/shard_map/ppermute | solution.py:440
  678.8 1.8 collective-permute-start.18
  682.4 53.4 %all_gather.13 = f32[16,2,12]{2,1,0:T(2,128)S(1)} all-gather(f32[1,2,12]{2,1,0:T(2,128)S(1)} %broadcast_select_fusion), channel_id=1, replica_groups=mesh['dp'=2,'cp'=8] {'dp','cp'}, dimensions={0}, use_global_device_ids=true | all-gather | bytes 1632 | tf_op jit(solution)/shard_map/all_gather | solution.py:482
  739.9 2.4 collective-permute-start.15
  742.8 64.6 %shard_map.99 = (bf16[4,256,6656]{2,1,0:T(8,128)(2,1)}, bf16[6656,6656]{1,0:T(8,128)(2,1)}) custom-call(s32[2]{0:T(128)} %get-tuple-element.84.idx_ref, bf16[256,1792]{1,0:T(8,128)(2,1)} %get-tuple-element.67.refs_0_, bf16[256,1536]{1,0:T(8,128)(2,1)} %get-tuple-element.68.refs_1_, ...), custom_call_target="tpu_custom_call", output_to_operand_aliasing={{1}: (8, {})} | custom-call | flops 22682796032 | bytes 177209344 | tf_op jit(solution)/shard_map/pallas_call | solution.py:409
  807.5 11.9 %collective-permute-done.13.refs_6_ = bf16[256,1792]{1,0:T(8,128)(2,1)} collective-permute-done((bf16[256,1792]{1,0:T(8,128)(2,1)}, bf16[256,1792]{1,0:T(8,128)(2,1)}, u32[]{:S(2)}, u32[]{:S(2)}) %collective-permute-start.13) | collective-permute-done | bytes 917536 | tf_op jit(solution)/shard_map/ppermute | solution.py:440
  819.3 90.3 %shard_map.100 = (bf16[4,256,6656]{2,1,0:T(8,128)(2,1)}, bf16[6656,6656]{1,0:T(8,128)(2,1)}) custom-call(s32[4]{0:T(128)} %pad_add_fusion.idx_ref, bf16[256,1792]{1,0:T(8,128)(2,1)} %collective-permute-done.7.refs_0_, bf16[256,1536]{1,0:T(8,128)(2,1)} %collective-permute-done.8.refs_1_, ...), custom_call_target="tpu_custom_call", output_to_operand_aliasing={{1}: (16, {}), {0}: (17, {})} | custom-call | flops 68048388096 | bytes 177209344 | tf_op jit(solution)/shard_map/pallas_call | solution.py:409
  (63 shorter events, 14.2 us)
Async XLA Ops:
  0.7 14.0 %copy-start.2 = (s32[256]{0:T(256)S(1)}, s32[256]{0:T(256)}, u32[]{:S(2)}) copy-start(s32[256]{0:T(256)} %param.7) | copy-start | bytes 3076
  9.9 4.7 copy-start
  9.9 165.1 %collective-permute-start.2 = (bf16[256,6656]{1,0:T(8,128)(2,1)}, bf16[256,6656]{1,0:T(8,128)(2,1)}, u32[]{:S(2)}, u32[]{:S(2)}) collective-permute-start(bf16[256,6656]{1,0:T(8,128)(2,1)} %get-tuple-element.77), channel_id=1, source_target_pairs={{0,2},{1,3},{2,0},{3,1},{4,6},{5,7},{6,4},{7,5},{8,10},{9,11},{10,... | collective-permute-start | bytes 10223624 | tf_op jit(solution)/shard_map/ppermute | solution.py:440
  13.1 162.2 %collective-permute-start = (bf16[256,6656]{1,0:T(8,128)(2,1)}, bf16[256,6656]{1,0:T(8,128)(2,1)}, u32[]{:S(2)}, u32[]{:S(2)}) collective-permute-start(bf16[256,6656]{1,0:T(8,128)(2,1)} %get-tuple-element.78), channel_id=1, source_target_pairs={{0,6},{1,7},{2,4},{3,5},{4,2},{5,3},{6,0},{7,1},{8,14},{9,15},{10,... | collective-permute-start | bytes 10223624 | tf_op jit(solution)/shard_map/ppermute | solution.py:440
  14.6 160.9 %collective-permute-start.4 = (bf16[256,6656]{1,0:T(8,128)(2,1)}, bf16[256,6656]{1,0:T(8,128)(2,1)}, u32[]{:S(2)}, u32[]{:S(2)}) collective-permute-start(bf16[256,6656]{1,0:T(8,128)(2,1)} %get-tuple-element.79), channel_id=1, source_target_pairs={{0,4},{1,5},{2,6},{3,7},{4,0},{5,1},{6,2},{7,3},{8,12},{9,13},{10,... | collective-permute-start | bytes 10223624 | tf_op jit(solution)/shard_map/ppermute | solution.py:440
  14.6 161.2 %collective-permute-start.6 = (bf16[256,6656]{1,0:T(8,128)(2,1)S(1)}, bf16[256,6656]{1,0:T(8,128)(2,1)}, u32[]{:S(2)}, u32[]{:S(2)}) collective-permute-start(bf16[256,6656]{1,0:T(8,128)(2,1)S(1)} %get-tuple-element.76.refs_0_), channel_id=1, source_target_pairs={{0,1},{1,0},{2,3},{3,2},{4,5},{5,4},{6,7},{7,6},{8,9},{9,8},{10,11... | collective-permute-start | bytes 10223624 | tf_op jit(solution)/shard_map/ppermute | solution.py:440
  175.0 82.5 %collective-permute-start.3 = (bf16[256,6656]{1,0:T(8,128)(2,1)}, bf16[256,6656]{1,0:T(8,128)(2,1)}, u32[]{:S(2)}, u32[]{:S(2)}) collective-permute-start(bf16[256,6656]{1,0:T(8,128)(2,1)} %collective-permute-done.2.refs_0_), channel_id=1, source_target_pairs={{0,1},{1,0},{2,3},{3,2},{4,5},{5,4},{6,7},{7,6},{8,9},{9,8},{10,11... | collective-permute-start | bytes 10223624 | tf_op jit(solution)/shard_map/ppermute | solution.py:440
  175.3 170.6 %collective-permute-start.1 = (bf16[256,6656]{1,0:T(8,128)(2,1)}, bf16[256,6656]{1,0:T(8,128)(2,1)}, u32[]{:S(2)}, u32[]{:S(2)}) collective-permute-start(bf16[256,6656]{1,0:T(8,128)(2,1)} %collective-permute-done.refs_0_.refs_4_), channel_id=1, source_target_pairs={{0,1},{1,0},{2,3},{3,2},{4,5},{5,4},{6,7},{7,6},{8,9},{9,8},{10,11... | collective-permute-start | bytes 10223624 | tf_op jit(solution)/shard_map/ppermute | solution.py:440
  175.5 82.0 %collective-permute-start.5 = (bf16[256,6656]{1,0:T(8,128)(2,1)}, bf16[256,6656]{1,0:T(8,128)(2,1)}, u32[]{:S(2)}, u32[]{:S(2)}) collective-permute-start(bf16[256,6656]{1,0:T(8,128)(2,1)} %collective-permute-done.4.refs_2_), channel_id=1, source_target_pairs={{0,1},{1,0},{2,3},{3,2},{4,5},{5,4},{6,7},{7,6},{8,9},{9,8},{10,11... | collective-permute-start | bytes 10223624 | tf_op jit(solution)/shard_map/ppermute | solution.py:440
  458.1 0.7 copy-start.1
  640.6 20.8 %collective-permute-start.8 = (bf16[256,1536]{1,0:T(8,128)(2,1)}, bf16[256,1536]{1,0:T(8,128)(2,1)}, u32[]{:S(2)}, u32[]{:S(2)}) collective-permute-start(bf16[256,1536]{1,0:T(8,128)(2,1)} %get-tuple-element.54), channel_id=1, source_target_pairs={{0,2},{1,3},{2,0},{3,1},{4,6},{5,7},{6,4},{7,5},{8,10},{9,11},{10,... | collective-permute-start | bytes 2359304 | tf_op jit(solution)/shard_map/ppermute | solution.py:440
  642.2 35.1 %collective-permute-start.10 = (bf16[256,1536]{1,0:T(8,128)(2,1)}, bf16[256,1536]{1,0:T(8,128)(2,1)}, u32[]{:S(2)}, u32[]{:S(2)}) collective-permute-start(bf16[256,1536]{1,0:T(8,128)(2,1)} %get-tuple-element.56), channel_id=1, source_target_pairs={{0,3},{1,2},{2,1},{3,0},{4,7},{5,6},{6,5},{7,4},{8,11},{9,10},{10,... | collective-permute-start | bytes 2359304 | tf_op jit(solution)/shard_map/ppermute | solution.py:440
  642.4 36.4 %collective-permute-start.12 = (bf16[256,1536]{1,0:T(8,128)(2,1)}, bf16[256,1536]{1,0:T(8,128)(2,1)}, u32[]{:S(2)}, u32[]{:S(2)}) collective-permute-start(bf16[256,1536]{1,0:T(8,128)(2,1)} %get-tuple-element.58), channel_id=1, source_target_pairs={{0,4},{1,5},{2,6},{3,7},{4,0},{5,1},{6,2},{7,3},{8,12},{9,13},{10,... | collective-permute-start | bytes 2359304 | tf_op jit(solution)/shard_map/ppermute | solution.py:440
  643.9 36.7 %collective-permute-start.14 = (bf16[256,1536]{1,0:T(8,128)(2,1)}, bf16[256,1536]{1,0:T(8,128)(2,1)}, u32[]{:S(2)}, u32[]{:S(2)}) collective-permute-start(bf16[256,1536]{1,0:T(8,128)(2,1)} %get-tuple-element.60), channel_id=1, source_target_pairs={{0,5},{1,4},{2,7},{3,6},{4,1},{5,0},{6,3},{7,2},{8,13},{9,12},{10,... | collective-permute-start | bytes 2359304 | tf_op jit(solution)/shard_map/ppermute | solution.py:440
  644.1 95.8 %collective-permute-start.7 = (bf16[256,1792]{1,0:T(8,128)(2,1)}, bf16[256,1792]{1,0:T(8,128)(2,1)}, u32[]{:S(2)}, u32[]{:S(2)}) collective-permute-start(bf16[256,1792]{1,0:T(8,128)(2,1)} %get-tuple-element.49), channel_id=1, source_target_pairs={{0,2},{1,3},{2,0},{3,1},{4,6},{5,7},{6,4},{7,5},{8,10},{9,11},{10,... | collective-permute-start | bytes 2752520 | tf_op jit(solution)/shard_map/ppermute | solution.py:440
  661.4 81.0 %collective-permute-start.19 = (bf16[256,1792]{1,0:T(8,128)(2,1)}, bf16[256,1792]{1,0:T(8,128)(2,1)}, u32[]{:S(2)}, u32[]{:S(2)}) collective-permute-start(bf16[256,1792]{1,0:T(8,128)(2,1)} %get-tuple-element.69), channel_id=1, source_target_pairs={{0,1},{1,0},{2,3},{3,2},{4,5},{5,4},{6,7},{7,6},{8,9},{9,8},{10,11... | collective-permute-start | bytes 2752520 | tf_op jit(solution)/shard_map/ppermute | solution.py:440
  677.3 60.5 %collective-permute-start.16 = (bf16[256,1536]{1,0:T(8,128)(2,1)}, bf16[256,1536]{1,0:T(8,128)(2,1)}, u32[]{:S(2)}, u32[]{:S(2)}) collective-permute-start(bf16[256,1536]{1,0:T(8,128)(2,1)} %get-tuple-element.62), channel_id=1, source_target_pairs={{0,6},{1,7},{2,4},{3,5},{4,2},{5,3},{6,0},{7,1},{8,14},{9,15},{10,... | collective-permute-start | bytes 2359304 | tf_op jit(solution)/shard_map/ppermute | solution.py:440
  678.8 59.6 %collective-permute-start.18 = (bf16[256,1536]{1,0:T(8,128)(2,1)}, bf16[256,1536]{1,0:T(8,128)(2,1)}, u32[]{:S(2)}, u32[]{:S(2)}) collective-permute-start(bf16[256,1536]{1,0:T(8,128)(2,1)} %get-tuple-element.64), channel_id=1, source_target_pairs={{0,7},{1,6},{2,5},{3,4},{4,3},{5,2},{6,1},{7,0},{8,15},{9,14},{10,... | collective-permute-start | bytes 2359304 | tf_op jit(solution)/shard_map/ppermute | solution.py:440
  680.6 59.2 %collective-permute-start.20 = (bf16[256,1536]{1,0:T(8,128)(2,1)}, bf16[256,1536]{1,0:T(8,128)(2,1)}, u32[]{:S(2)}, u32[]{:S(2)}) collective-permute-start(bf16[256,1536]{1,0:T(8,128)(2,1)} %get-tuple-element.70), channel_id=1, source_target_pairs={{0,1},{1,0},{2,3},{3,2},{4,5},{5,4},{6,7},{7,6},{8,9},{9,8},{10,11... | collective-permute-start | bytes 2359304 | tf_op jit(solution)/shard_map/ppermute | solution.py:440
  737.9 69.6 %collective-permute-start.9 = (bf16[256,1792]{1,0:T(8,128)(2,1)}, bf16[256,1792]{1,0:T(8,128)(2,1)}, u32[]{:S(2)}, u32[]{:S(2)}) collective-permute-start(bf16[256,1792]{1,0:T(8,128)(2,1)} %get-tuple-element.55), channel_id=1, source_target_pairs={{0,3},{1,2},{2,1},{3,0},{4,7},{5,6},{6,5},{7,4},{8,11},{9,10},{10,... | collective-permute-start | bytes 2752520 | tf_op jit(solution)/shard_map/ppermute | solution.py:440
  738.4 69.0 %collective-permute-start.11 = (bf16[256,1792]{1,0:T(8,128)(2,1)}, bf16[256,1792]{1,0:T(8,128)(2,1)}, u32[]{:S(2)}, u32[]{:S(2)}) collective-permute-start(bf16[256,1792]{1,0:T(8,128)(2,1)} %get-tuple-element.57), channel_id=1, source_target_pairs={{0,4},{1,5},{2,6},{3,7},{4,0},{5,1},{6,2},{7,3},{8,12},{9,13},{10,... | collective-permute-start | bytes 2752520 | tf_op jit(solution)/shard_map/ppermute | solution.py:440
  739.9 79.5 %collective-permute-start.13 = (bf16[256,1792]{1,0:T(8,128)(2,1)}, bf16[256,1792]{1,0:T(8,128)(2,1)}, u32[]{:S(2)}, u32[]{:S(2)}) collective-permute-start(bf16[256,1792]{1,0:T(8,128)(2,1)} %get-tuple-element.59), channel_id=1, source_target_pairs={{0,5},{1,4},{2,7},{3,6},{4,1},{5,0},{6,3},{7,2},{8,13},{9,12},{10,... | collective-permute-start | bytes 2752520 | tf_op jit(solution)/shard_map/ppermute | solution.py:440
  739.9 79.4 %collective-permute-start.15 = (bf16[256,1792]{1,0:T(8,128)(2,1)}, bf16[256,1792]{1,0:T(8,128)(2,1)}, u32[]{:S(2)}, u32[]{:S(2)}) collective-permute-start(bf16[256,1792]{1,0:T(8,128)(2,1)} %get-tuple-element.61), channel_id=1, source_target_pairs={{0,6},{1,7},{2,4},{3,5},{4,2},{5,3},{6,0},{7,1},{8,14},{9,15},{10,... | collective-permute-start | bytes 2752520 | tf_op jit(solution)/shard_map/ppermute | solution.py:440
  742.4 77.0 %collective-permute-start.17 = (bf16[256,1792]{1,0:T(8,128)(2,1)}, bf16[256,1792]{1,0:T(8,128)(2,1)}, u32[]{:S(2)}, u32[]{:S(2)}) collective-permute-start(bf16[256,1792]{1,0:T(8,128)(2,1)} %get-tuple-element.63), channel_id=1, source_target_pairs={{0,7},{1,6},{2,5},{3,4},{4,3},{5,2},{6,1},{7,0},{8,15},{9,14},{10,... | collective-permute-start | bytes 2752520 | tf_op jit(solution)/shard_map/ppermute | solution.py:440
